TPU v7x, 32 devices: a whole 2x2x4 slice. The times are simulated.
32 devices in a mesh: req: 8 (over y, x, core), head: 4 (over z).
Axes of the slice: x: 2, y: 2, z: 4, core: 2. Of those that a mesh axis runs over, the one named last changes fastest.
Arguments:
- queries: bfloat16 [128, 64, 128], P('req', 'head'), may hold values from -6 to 6
- k_codes: bfloat16 [8192, 16, 8, 128], P('req', None, 'head'), may hold values from -6 to 6
- value_quantized_codes: bfloat16 [8192, 16, 8, 128], P('req', None, 'head'), may hold values from -6 to 6
- key_page_scale: float32 [8192, 8], P('req', 'head'), may hold values from 0.5 to 2
- value_page_scale: float32 [8192, 8], P('req', 'head'), may hold values from 4 to 16
- lengths: int32 [128], P('req'), may hold values from 1 to 2032
- page_table: int32 [128, 128], P('req'), may hold values from -1 to 8191, as said below
- out_weight: bfloat16 [8192, 8192], P('head', 'req'), may hold values from -0.0625 to 0.0625
Outputs:
- attn_out: bfloat16 [128, 8192], P(None, ('req', 'head'))
Inputs may be any that keep to these rules, and one draw needn't show every extreme that they name: `page_table`: entries j below ceil(lengths[r] / 16) name pool pages; all such entries of all requests together name every pool page exactly once. Entries beyond are -1.
All inputs are finite; a program needn't handle non-finite values.
Results may differ from a plain program's by a relative error of at most 0.02.
Values may be sent and summed in bfloat16 or wider, within the bound.
A program may use at most 128 MiB of HBM per device.

v0:
```python
import functools
import math

import jax
import jax.numpy as jnp
from jax import lax
from jax.experimental import pallas as pl
from jax.experimental.pallas import tpu as pltpu
from jax.sharding import PartitionSpec as P

floor_score = -1e30
DIGIT = 32
GROUP = 8
LANES = 128


def locate_kernel(page_size, table_ref, lengths_ref, out_ref, acc):
    requests, width = table_ref.shape
    rows = out_ref.shape[0]
    step = 8
    acc[...] = jnp.zeros_like(acc)
    iota_hi = lax.broadcasted_iota(jnp.int32, (rows, width), 0)
    iota_lo = lax.broadcasted_iota(jnp.int32, (DIGIT, width), 0)
    entry = lax.broadcasted_iota(jnp.int32, (1, width), 1) * page_size

    def body(i, carry):
        lefts, rights = [], []
        block = table_ref[pl.ds(pl.multiple_of(i * step, step), step), :]
        for s in range(step):
            r = i * step + s
            row = block[s : s + 1, :]
            hi = row >> 5
            lo = row & (DIGIT - 1)
            live = jnp.minimum(lengths_ref[r] - entry, page_size).astype(jnp.float32)
            lefts.append(jnp.where(iota_hi == hi, 1.0, 0.0).astype(jnp.bfloat16))
            same = iota_lo == lo
            r_high = (r // 256).astype(jnp.float32)
            r_low = (r % 256).astype(jnp.float32)
            parts = [
                jnp.where(same, r_high, 0.0),
                jnp.where(same, r_low, 0.0),
                jnp.where(same, live, 0.0),
            ]
            rights.append(jnp.concatenate(parts, axis=0).astype(jnp.bfloat16))
        left = jnp.concatenate(lefts, axis=1)
        right = jnp.concatenate(rights, axis=1)
        acc[...] += lax.dot_general(
            left, right, (((1,), (1,)), ((), ())), preferred_element_type=jnp.float32
        )
        return carry

    lax.fori_loop(0, requests // step, body, 0)
    out_ref[...] = acc[...]


def attend_kernel(
    kv_local,
    q_ref,
    member_ref,
    scale_ref,
    bias_ref,
    block_ref,
    vscale_ref,
    k_ref,
    v_ref,
    out_ref,
    q_rows,
    m_rows,
    sums,
    shift,
    extra,
):
    heads, pages, dim = q_rows.shape
    requests = q_ref.shape[0]
    group_rows = block_ref.shape[1]
    per_head = heads // kv_local
    steps = pl.num_programs(0)
    pid = pl.program_id(0)
    groups = k_ref.shape[0] // group_rows

    @pl.when(pid == 0)
    def _():
        member = member_ref[...].astype(jnp.bfloat16)

        def pick(i, carry):
            cols = q_ref[:, pl.ds(pl.multiple_of(i * 2 * dim, 2 * dim), 2 * dim)]
            got = jnp.dot(member, cols, preferred_element_type=jnp.float32)
            q_rows[2 * i] = got[:, :dim]
            q_rows[2 * i + 1] = got[:, dim:]
            return carry

        lax.fori_loop(0, heads // 2, pick, 0)

    def group(i, carry):
        g = pid * groups + i
        p0 = pl.multiple_of(g * GROUP, GROUP)
        q = jnp.concatenate([q_rows[h, pl.ds(p0, GROUP), :] for h in range(heads)], axis=0)
        start = pl.multiple_of(i * group_rows, group_rows)
        kk = k_ref[pl.ds(start, group_rows), :]
        vv = v_ref[pl.ds(start, group_rows), :]
        s = lax.dot_general(
            q.astype(jnp.bfloat16), kk, (((1,), (1,)), ((), ())), preferred_element_type=jnp.float32
        )
        s = (s * scale_ref[pl.ds(g, 1), :] + bias_ref[pl.ds(g, 1), :]) + block_ref[...]
        top = jnp.max(s, axis=1, keepdims=True)
        w = jnp.exp(s - top).astype(jnp.bfloat16)
        both = jnp.concatenate([vv, jnp.ones_like(vv)], axis=1)
        o = jnp.dot(w, both, preferred_element_type=jnp.float32)
        factors = [vscale_ref[pl.ds(p0, GROUP), k : k + 1] for k in range(kv_local)]
        for h in range(heads):
            rows = slice(h * GROUP, (h + 1) * GROUP)
            sums[h, pl.ds(p0, GROUP), :dim] = o[rows, :dim] * factors[h // per_head]
            sums[h, pl.ds(p0, GROUP), dim:] = o[rows, dim:]
            m_rows[h, pl.ds(p0, GROUP), :] = jnp.broadcast_to(top[rows], (GROUP, dim))
        return carry

    lax.fori_loop(0, groups, group, 0, unroll=4)

    @pl.when(pid == steps - 1)
    def _():
        shift[...] = jnp.zeros_like(shift)
        extra[...] = jnp.zeros_like(extra)
        lane = lax.broadcasted_iota(jnp.int32, extra.shape, 1)

        def finish(h, carry):
            inside = member_ref[...] > 0.5
            top = jnp.concatenate([m_rows[h]] * (requests // dim), axis=1)
            peak = jnp.max(jnp.where(inside, top, floor_score), axis=0, keepdims=True)
            peak = peak.astype(jnp.bfloat16).astype(jnp.float32)
            f = jnp.where(inside, jnp.exp(top - peak), 0.0).astype(jnp.bfloat16)
            got = lax.dot_general(
                f,
                sums[h].astype(jnp.bfloat16),
                (((0,), (0,)), ((), ())),
                preferred_element_type=jnp.float32,
            )
            cols = pl.ds(pl.multiple_of(h * dim, dim), dim)
            out_ref[:, cols] = got[:, :dim].astype(jnp.bfloat16)
            den = got[:, dim:]
            den_high = den.astype(jnp.bfloat16).astype(jnp.float32)
            kept = jnp.where(lane == h, den_high, extra[...])
            extra[...] = jnp.where(lane == heads + h, den - den_high, kept)
            shift[pl.ds(2 * heads + h, 1), :] = peak
            return carry

        lax.fori_loop(0, heads, finish, 0)
        tail = jnp.where(lane < 2 * heads, extra[...], shift[...].T)
        out_ref[:, heads * dim :] = tail.astype(jnp.bfloat16)


def on_device(
    queries,
    k_codes,
    value_quantized_codes,
    key_page_scale,
    value_page_scale,
    lengths,
    page_table,
    out_weight,
):
    pages, page_size, kv_local, dim = k_codes.shape
    rows_here, heads, _ = queries.shape
    per_head = heads // kv_local
    width = heads * dim
    vmem = pl.BlockSpec(memory_space=pltpu.VMEM)
    smem = pl.BlockSpec(memory_space=pltpu.SMEM)

    table = lax.all_gather(page_table, "req", axis=0, tiled=True)
    all_lengths = lax.all_gather(lengths, "req", axis=0, tiled=True)
    q_all = lax.all_gather(queries.reshape(rows_here, width), "req", axis=0, tiled=True)
    requests = table.shape[0]
    sources = lax.axis_size("req")
    local_table = table - lax.axis_index("req") * pages

    found = pl.pallas_call(
        functools.partial(locate_kernel, page_size),
        out_shape=jax.ShapeDtypeStruct((pages // DIGIT, 3 * DIGIT), jnp.float32),
        in_specs=[vmem, smem],
        out_specs=vmem,
        scratch_shapes=[pltpu.VMEM((pages // DIGIT, 3 * DIGIT), jnp.float32)],
        name="locate",
    )(local_table, all_lengths)
    owner = (found[:, :DIGIT] * 256.0 + found[:, DIGIT : 2 * DIGIT]).reshape(pages)
    live = found[:, 2 * DIGIT :].reshape(pages)
    ids = jnp.arange(requests, dtype=jnp.int32).astype(jnp.float32)
    member = (owner[:, None] == ids[None, :]).astype(jnp.float32)

    page_rows = page_size * kv_local
    group_rows = GROUP * page_rows
    token = jnp.arange(page_size, dtype=jnp.int32).astype(jnp.float32)[None, :, None]
    full = (pages, page_size, kv_local)
    bias = jnp.where(jnp.broadcast_to(token < live[:, None, None], full), 0.0, floor_score)
    bias = bias.reshape(pages // GROUP, group_rows)
    scale = jnp.broadcast_to(key_page_scale[:, None, :] / math.sqrt(dim), full)
    scale = scale.reshape(pages // GROUP, group_rows)
    row = jnp.arange(heads * GROUP, dtype=jnp.int32)[:, None]
    col = jnp.arange(group_rows, dtype=jnp.int32)[None, :]
    same = (row % GROUP == col // page_rows) & (row // GROUP // per_head == col % kv_local)
    block = jnp.where(same, 0.0, floor_score).astype(jnp.float32)

    k_rows = k_codes.reshape(pages * page_rows, dim)
    v_rows = value_quantized_codes.reshape(pages * page_rows, dim)
    block_pages = 128
    steps = pages // block_pages
    whole = lambda shape: pl.BlockSpec(shape, lambda i: (0,) * len(shape))
    stream = pl.BlockSpec((block_pages * page_rows, dim), lambda i: (i, 0))
    partial_sums = pl.pallas_call(
        functools.partial(attend_kernel, kv_local),
        grid=(steps,),
        out_shape=jax.ShapeDtypeStruct((requests, width + LANES), jnp.bfloat16),
        in_specs=[vmem, vmem, vmem, vmem, vmem, vmem, stream, stream],
        out_specs=whole((requests, width + LANES)),
        scratch_shapes=[
            pltpu.VMEM((heads, pages, dim), jnp.float32),
            pltpu.VMEM((heads, pages, dim), jnp.float32),
            pltpu.VMEM((heads, pages, 2 * dim), jnp.float32),
            pltpu.VMEM((LANES, requests), jnp.float32),
            pltpu.VMEM((requests, LANES), jnp.float32),
        ],
        compiler_params=pltpu.CompilerParams(
            vmem_limit_bytes=60 * 1024 * 1024, dimension_semantics=("arbitrary",)
        ),
        name="attend",
    )(q_all, member, scale, bias, block, value_page_scale, k_rows, v_rows)

    got = lax.all_to_all(
        partial_sums.reshape(sources, rows_here, width + LANES),
        "req",
        split_axis=0,
        concat_axis=0,
        tiled=True,
    ).astype(jnp.float32)
    tail = got[:, :, width:]
    den = tail[:, :, :heads] + tail[:, :, heads : 2 * heads]
    peak = tail[:, :, 2 * heads : 3 * heads]
    factor = jnp.exp(peak - jnp.max(peak, axis=0)[None])
    factor = factor / jnp.sum(den * factor, axis=0)[None]
    numer = got[:, :, :width].reshape(sources, rows_here, heads, dim)
    attention = jnp.sum(numer * factor[..., None], axis=0).reshape(rows_here, width)
    terms = jnp.dot(
        lax.all_gather(attention.astype(jnp.bfloat16), "req", axis=0, tiled=True),
        out_weight,
        preferred_element_type=jnp.float32,
    )
    return lax.psum_scatter(terms.astype(jnp.bfloat16), "head", scatter_dimension=1, tiled=True)


def solution(mesh):
    in_specs = (
        P("req", "head", None),
        P("req", None, "head", None),
        P("req", None, "head", None),
        P("req", "head"),
        P("req", "head"),
        P("req"),
        P("req", None),
        P("head", "req"),
    )
    out_specs = P(None, ("req", "head"))
    return jax.shard_map(
        on_device, mesh=mesh, in_specs=in_specs, out_specs=out_specs, check_vma=False
    )
```

profile of v0, /device:TPU:0, one launch (start us, length us, event | category | flops | bytes accessed | tf_op | source)
XLA Modules:
  0.0 156.7 jit_solution(17408326440663370600)
XLA Ops:
  6.6 10.9 %all_gather.13 = s32[128,128]{1,0:T(8,128)S(1)} all-gather(s32[16,128]{1,0:T(8,128)} %param.14), channel_id=1, replica_groups=mesh['req'=8,'head'=4] {'req'}, dimensions={0}, use_global_device_ids=true | all-gather | bytes 73728 | tf_op jit(solution)/shard_map/all_gather | solution.py:168
  17.5 1.2 dynamic-slice
  19.4 0.9 dynamic-update-slice
  20.2 7.7 %all-reduce.lengths_ref = s32[128]{0:T(128)} all-reduce(s32[128]{0:T(128)S(1)} %dynamic-update-slice), channel_id=1, replica_groups=mesh['req'=8,'head'=4] {'req'}, use_global_device_ids=true, to_apply=%add | all-reduce | flops 128 | bytes 1024
  27.9 0.6 broadcast_subtract_fusion.table_ref
  28.5 4.6 %locate.1 = f32[32,96]{1,0:T(8,128)} custom-call(s32[128,128]{1,0:T(8,128)} %broadcast_subtract_fusion.table_ref, s32[128]{0:T(128)} %all-reduce.lengths_ref), custom_call_target="tpu_custom_call" | custom-call | tf_op jit(solution)/shard_map/locate/pallas_call | solution.py:175
  33.1 0.9 fusion.4
  34.1 0.2 compare_select_fusion
  34.3 5.9 %broadcast_in_dim.37 = f32[1024,16,2]{2,1,0:T(8,128)} broadcast(f32[1024,16]{1,0:T(8,128)S(1)} %compare_select_fusion), dimensions={0,1} | broadcast | bytes 196608 | tf_op jit(solution)/shard_map/broadcast_in_dim | solution.py:192
  40.2 7.5 %reshape.212.bias_ref = f32[128,256]{1,0:T(8,128)} reshape(f32[1024,16,2]{2,1,0:T(8,128)} %broadcast_in_dim.37) | data formatting | bytes 262144 | tf_op jit(solution)/shard_map/reshape | solution.py:193
  47.7 0.2 copy.11
  48.0 3.8 %broadcast_in_dim.20 = f32[1024,16,2]{2,1,0:T(8,128)} broadcast(f32[1024,2]{1,0:T(8,128)S(1)} %copy.11), dimensions={0,2} | broadcast | bytes 139264 | tf_op jit(solution)/shard_map/broadcast_in_dim | solution.py:194
  51.7 7.5 %reshape.211.scale_ref = f32[128,256]{1,0:T(8,128)} reshape(f32[1024,16,2]{2,1,0:T(8,128)} %broadcast_in_dim.20) | data formatting | bytes 262144 | tf_op jit(solution)/shard_map/reshape | solution.py:195
  59.2 10.5 %all_gather.12.q_ref = bf16[128,2048]{1,0:T(8,128)(2,1)} all-gather(bf16[16,2048]{1,0:T(8,128)(2,1)S(1)} %bitcast.15), channel_id=1, replica_groups=mesh['req'=8,'head'=4] {'req'}, dimensions={0}, use_global_device_ids=true | all-gather | bytes 589824 | tf_op jit(solution)/shard_map/all_gather | solution.py:170
  69.7 1.0 copy.12.vscale_ref
  70.8 1.0 compare_convert_fusion.member_ref
  71.8 0.8 and_select_fusion.block_ref
  72.6 29.9 %attend.1 = bf16[128,2176]{1,0:T(8,128)(2,1)} custom-call(bf16[128,2048]{1,0:T(8,128)(2,1)} %all_gather.12.q_ref, f32[1024,128]{1,0:T(8,128)} %compare_convert_fusion.member_ref, f32[128,256]{1,0:T(8,128)} %reshape.211.scale_ref, f32[128,256]{1,0:T(8,128)} %reshape.212.bias_ref, f32[128,256]{1,0:T(8,128)} %and_select_fusion.block_ref, ...), custom_call_target="tpu_custom_call" | custom-call | tf_op jit(solution)/shard_map/attend/pallas_call | solution.py:207
  102.4 13.5 %all_to_all.5 = bf16[8,16,2176]{2,1,0:T(8,128)(2,1)S(1)} all-to-all(bf16[8,16,2176]{2,1,0:T(8,128)(2,1)} %bitcast.14), channel_id=1, replica_groups=mesh['req'=8,'head'=4] {'req'}, dimensions={0} | all-to-all | bytes 1114112 | tf_op jit(solution)/shard_map/all_to_all | solution.py:226
  116.3 0.3 mul.27
  116.6 0.2 mul.28
  116.9 8.9 %all_gather.15 = bf16[128,2048]{1,0:T(8,128)(2,1)S(1)} all-gather(bf16[16,2048]{1,0:T(8,128)(2,1)S(1)} %fusion), channel_id=1, replica_groups=mesh['req'=8,'head'=4] {'req'}, dimensions={0}, use_global_device_ids=true | all-gather | bytes 589824 | tf_op jit(solution)/shard_map/all_gather | solution.py:241
  125.8 3.6 %convolution_convert_fusion = bf16[128,1024]{1,0:T(8,128)(2,1)} fusion(bf16[128,2048]{1,0:T(8,128)(2,1)S(1)} %all_gather.15, bf16[2048,1024]{1,0:T(8,128)(2,1)} %param.15), kind=kOutput, calls=%fused_computation | convolution fusion | flops 537001984 | bytes 4980736 | tf_op jit(solution)/shard_map/dot_general | solution.py:240
  129.5 20.4 %reduce-scatter.2.cloned.1.call-done = bf16[128,256]{1,0:T(8,128)(2,1)} async-done(((bf16[128,1024]{1,0:T(8,128)(2,1)}), bf16[128,256]{1,0:T(8,128)(2,1)}) %reduce-scatter.2.cloned.1.call-update) | async-done | bytes 65552 | tf_op jit(solution)/shard_map/reduce_scatter | solution.py:245
  (22 shorter events, 0.7 us)
Async XLA Ops:
  6.5 143.4 %reduce-scatter.2.cloned.1.call-start = ((), (), s32[]{:S(2)}) async-start(), calls=%async_computation.2 | async-start | bytes 327680 | tf_op jit(solution)/shard_map/reduce_scatter | solution.py:245
  40.2 7.5 %copy-start.2 = (f32[1024,2]{0,1:T(2,128)S(1)}, f32[1024,2]{0,1:T(2,128)}, u32[]{:S(2)}) copy-start(f32[1024,2]{0,1:T(2,128)} %param.11) | copy-start | bytes 24580
  51.7 7.5 %copy-start = (bf16[16,16,128]{2,1,0:T(8,128)(2,1)S(1)}, bf16[16,16,128]{2,1,0:T(8,128)(2,1)}, u32[]{:S(2)}) copy-start(bf16[16,16,128]{2,1,0:T(8,128)(2,1)} %param.8) | copy-start | bytes 196612
  51.7 18.0 %copy-start.1 = (f32[1024,2]{0,1:T(2,128)S(1)}, f32[1024,2]{0,1:T(2,128)}, u32[]{:S(2)}) copy-start(f32[1024,2]{0,1:T(2,128)} %param.12) | copy-start | bytes 24580
Sparse Core Ops, SparseCore 0:
  129.6 20.2 reduce-scatter.1
where the time goes:
time: 157 us
  blocking collectives  51.5 us (33%)
  Pallas kernels  34.4 us (22%)
  local copies, waits for them, and re-layouts  28.6 us (18%)
  waiting for transfers between devices  20.4 us (13%)
  between operations  14.2 us (9%)
  other arithmetic  3.99 us (3%)
  matrix products  3.64 us (2%)
    pallas_call x1, Pallas kernels, on_device(): pl.pallas_call(functools.partial(attend_kernel, kv_local), grid=(steps,),...  29.9 us
    reduce_scatter x1, waiting for transfers between devices, on_device(): lax.psum_scatter(terms.astype(jnp.bfloat16), 'head', scatter_dimension=1,...  20.4 us
    all_to_all x1, blocking collectives, on_device(): lax.all_to_all(partial_sums.reshape(sources, rows_here, width + LANES), '...  13.5 us
    all_gather x1, blocking collectives, on_device(): table = lax.all_gather(page_table, 'req', axis=0, tiled=True)  10.9 us
    all_gather x1, blocking collectives, on_device(): lax.all_gather(queries.reshape(rows_here, width), 'req', axis=0, tiled=True)  10.5 us
    all_gather x1, blocking collectives, on_device(): lax.all_gather(attention.astype(jnp.bfloat16), 'req', axis=0, tiled=True)  8.9 us
    unnamed x1, blocking collectives  7.68 us
    reshape x1, local copies, waits for them, and re-layouts, on_device(): scale = scale.reshape(pages // GROUP, group_rows)  7.48 us
  transfers between devices with their start and end apart: 1, of which 1 were waited for; matrix products, arithmetic and copies ran while one was open for 0% of the time, Pallas kernels for 0%

commit v1 on v0

v1 whole, which is shorter than its diff:
```python
import functools
import math

import jax
import jax.numpy as jnp
from jax import lax
from jax.experimental import pallas as pl
from jax.experimental.pallas import tpu as pltpu
from jax.sharding import PartitionSpec as P

MESH = pl.DeviceIdType.MESH
FLOOR = -1e30
DROP = -3e38
LANES = 128
SUB = 8
LIVE_BITS = 5
ROUND = 8
F32 = jnp.float32
BF16 = jnp.bfloat16
I32 = jnp.int32


def nt(a, b):
    return lax.dot_general(a, b, (((1,), (1,)), ((), ())), preferred_element_type=F32)


def nn(a, b):
    return jnp.dot(a, b, preferred_element_type=F32)


def iota(shape, axis):
    return lax.broadcasted_iota(I32, shape, axis)


def list_kernel(cfg, lengths_ref, table_ref, out_ref):
    sources, rows_here, pages = cfg["sources"], cfg["rows_here"], cfg["pages"]
    page_size, per_group = cfg["page_size"], cfg["per_group"]
    slot_rows, group_rows = cfg["slot_rows"], cfg["group_rows"]
    shape = (rows_here, LANES)
    row_id = iota(shape, 0)
    lengths = jnp.zeros(shape, I32)
    for r in range(rows_here):
        lengths = jnp.where(row_id == r, lengths_ref[r], lengths)
    live = jnp.minimum(lengths - iota(shape, 1) * page_size, page_size)
    table = table_ref[...]
    locals_, mines = [], []
    for d in range(sources):
        local = table - d * pages
        locals_.append(local)
        mines.append((live > 0) & (local >= 0) & (local < pages))
    flag = jnp.concatenate([jnp.where(m, 1.0, 0.0) for m in mines], axis=0).astype(BF16)
    total = sources * rows_here
    up = jnp.where(iota((LANES, LANES), 0) < iota((LANES, LANES), 1), 1.0, 0.0).astype(BF16)
    before = nn(flag, up)
    count = nn(flag, jnp.ones((LANES, LANES), BF16))
    need = jnp.floor((count + (per_group - 1)) * (1.0 / per_group))
    i, j = iota((total, total), 0), iota((total, total), 1)
    tri = jnp.where((i >= j) & (i // rows_here == j // rows_here), 1.0, 0.0).astype(BF16)
    ends = nn(tri, need.astype(BF16))
    starts = ends - need
    slots = (starts * per_group + before).astype(I32)

    key = jnp.full(shape, -1, I32)
    page = jnp.zeros(shape, I32)
    for d in range(sources):
        slot = slots[d * rows_here : (d + 1) * rows_here] + d * (slot_rows * LANES)
        key = jnp.where(mines[d], slot, key)
        page = jnp.where(mines[d], locals_[d], page)
    one = (page >> 2).astype(F32)
    two = ((page & 3) * (1 << LIVE_BITS) + live).astype(F32)
    high, low = key >> 7, key & (LANES - 1)
    hi_rows = -(-(sources * slot_rows) // 16) * 16
    hi_iota, lo_iota = iota((hi_rows, LANES), 0), iota((LANES, LANES), 0)
    lefts, rights = [], []
    for r in range(rows_here):
        row = slice(r, r + 1)
        lefts.append(jnp.where(hi_iota == high[row], 1.0, 0.0).astype(BF16))
        same = lo_iota == low[row]
        pair = [jnp.where(same, one[row], 0.0), jnp.where(same, two[row], 0.0)]
        rights.append(jnp.concatenate(pair, axis=0).astype(BF16))
    found = nt(jnp.concatenate(lefts, axis=1), jnp.concatenate(rights, axis=1))
    found = (found[:, :LANES] * float(4 << LIVE_BITS) + found[:, LANES:]).astype(I32)

    lane = iota(shape, 1).astype(F32)
    diag = row_id == iota(shape, 1)
    for d in range(sources):
        rows = slice(d * rows_here, (d + 1) * rows_here)
        end, begin, some = ends[rows], starts[rows], need[rows] > 0.5
        out_ref[d, :slot_rows, :] = found[d * slot_rows : (d + 1) * slot_rows]
        for b in range(group_rows):
            here = lane + float(b * LANES)
            done = end <= here
            owner = jnp.sum(jnp.where(done, 1.0, 0.0), axis=0, keepdims=True)
            owner = jnp.minimum(owner, float(rows_here - 1))
            last = jnp.min(jnp.where(done, 4096.0, end), axis=0, keepdims=True) - 1.0
            opens = jnp.where((begin == here) & some, 1.0, 0.0)
            opens = jnp.max(opens, axis=0, keepdims=True)
            value = (last * 2.0 + (1.0 - opens)) * float(rows_here) + owner
            out_ref[d, slot_rows + b : slot_rows + b + 1, :] = value.astype(I32)
        mark = jnp.maximum(end - 1.0, 0.0) * 2.0 + jnp.where(some, 1.0, 0.0)
        mark = jnp.sum(jnp.where(diag, mark, 0.0), axis=0, keepdims=True)
        size = jnp.maximum(jnp.max(end, axis=0, keepdims=True), 1.0)
        mark = jnp.where(iota((1, LANES), 1) == rows_here, size, mark)
        base = slot_rows + group_rows
        out_ref[d, base : base + 1, :] = mark.astype(I32)


def kernel(
    cfg,
    info_ref,
    kscale_ref,
    vscale_ref,
    q_hbm,
    k_hbm,
    v_hbm,
    w_hbm,
    out_ref,
    info_all,
    info,
    q_all,
    k_buf,
    v_buf,
    w_buf,
    kse,
    vse,
    scores,
    peaks,
    dens,
    accs,
    num_send,
    lse_send,
    num_recv,
    lse_recv,
    mixed,
    att_all,
    term_send,
    term_recv,
    q_sem,
    load_sems,
    info_sem,
    smem_sem,
    t_send,
    t_recv,
    q_send,
    q_recv,
    n_send,
    n_recv,
    l_send,
    l_recv,
    a_send,
    a_recv,
    z_send,
    z_recv,
):
    sources, nz = cfg["sources"], cfg["nz"]
    rows_here, heads, dim = cfg["rows_here"], cfg["heads"], cfg["dim"]
    pages, page_rows, page_size = cfg["pages"], cfg["page_rows"], cfg["page_size"]
    requests = rows_here * sources
    kv_local = page_rows // page_size
    per_group = LANES // page_rows
    n_groups = cfg["n_groups"]
    steps = n_groups // ROUND
    width = heads * dim
    me = lax.axis_index("req")
    mz = lax.axis_index("head")
    slot_rows, mark_row = cfg["slot_rows"], cfg["slot_rows"] + cfg["group_rows"]

    q_load = pltpu.make_async_copy(q_hbm, q_all.at[pl.ds(me * rows_here, rows_here)], q_sem)
    q_load.start()
    info_load = pltpu.make_async_copy(info_ref.at[me], info_all.at[me], info_sem)
    info_load.start()
    loads = []
    parts = load_sems.shape[1]
    for which, (src, dst) in enumerate(((k_hbm, k_buf), (v_hbm, v_buf), (w_hbm, w_buf))):
        chunk = src.shape[0] // parts
        for c in range(parts):
            rows = pl.ds(c * chunk, chunk)
            cp = pltpu.make_async_copy(src.at[rows], dst.at[rows], load_sems.at[which, c])
            cp.start()
            loads.append(cp)
    k_loads, v_loads, w_loads = loads[:parts], loads[parts : 2 * parts], loads[2 * parts :]

    barrier = pltpu.get_barrier_semaphore()
    for k in range(1, sources):
        pl.semaphore_signal(
            barrier, inc=1, device_id={"req": lax.rem(me + k, sources)}, device_id_type=MESH
        )
    for k in range(1, nz):
        pl.semaphore_signal(barrier, inc=1, device_id={"head": lax.rem(mz + k, nz)}, device_id_type=MESH)
    pl.semaphore_wait(barrier, sources + nz - 2)

    def info_copy(peer, owner):
        return pltpu.make_async_remote_copy(
            src_ref=info_ref.at[peer],
            dst_ref=info_all.at[owner],
            send_sem=t_send.at[peer],
            recv_sem=t_recv.at[owner],
            device_id={"req": peer},
            device_id_type=MESH,
        )

    def q_copy(k, owner):
        peer = lax.rem(me + k, sources)
        rows = pl.ds(owner * rows_here, rows_here)
        return pltpu.make_async_remote_copy(
            src_ref=q_all.at[rows],
            dst_ref=q_all.at[rows],
            send_sem=q_send.at[peer],
            recv_sem=q_recv.at[owner],
            device_id={"req": peer},
            device_id_type=MESH,
        )

    for k in range(1, sources):
        info_copy(lax.rem(me + k, sources), me).start()
    q_load.wait()
    for k in range(1, sources):
        q_copy(k, me).start()

    lane_sub = iota((LANES, LANES), 0)
    for src, dst, factor in ((kscale_ref, kse, 1.0 / math.sqrt(dim)), (vscale_ref, vse, 1.0)):
        for b in range(pages // LANES):
            cols = slice(b * LANES, (b + 1) * LANES)
            both = src[kv_local - 1 : kv_local, cols]
            for v in range(kv_local - 1):
                both = jnp.where(lane_sub % kv_local == v, src[v : v + 1, cols], both)
            both = jnp.broadcast_to(both * factor, (LANES, LANES)).T
            dst[b * LANES : (b + 1) * LANES, 0, :] = both

    info_load.wait()
    for k in range(1, sources):
        peer = lax.rem(me + k, sources)
        info_copy(peer, peer).wait_recv()
    to_smem = pltpu.make_async_copy(info_all, info, smem_sem)
    to_smem.start()
    to_smem.wait()
    for k in range(1, sources):
        q_copy(k, lax.rem(me + k, sources)).wait_recv()
    for cp in k_loads:
        cp.wait()

    lane8 = iota((SUB, LANES), 1)
    token = (lane8 % page_rows) // kv_local
    per_head = heads // kv_local
    kv_masks = [lane8 % kv_local == (t * SUB) // per_head for t in range(heads // SUB)]
    blank = jnp.zeros((heads, dim), BF16)

    def by_page(parts):
        got = parts[per_group - 1]
        for i in range(per_group - 2, -1, -1):
            got = jnp.where(lane8 < (i + 1) * page_rows, parts[i], got)
        return got

    def page_of(at, i):
        src, k = at
        lane_at = (k & (LANES // per_group - 1)) * per_group
        value = info[src, k // (LANES // per_group), lane_at + i]
        return value >> LIVE_BITS, value & ((1 << LIVE_BITS) - 1)

    def group_of(at):
        src, k = at
        value = info[src, slot_rows + k // LANES, k & (LANES - 1)]
        owner = src * rows_here + (value & (rows_here - 1))
        rest = value // rows_here
        return owner, (rest & 1).astype(F32), rest // 2

    def advance(at):
        src, k = at
        more = k + 1 < info[src, mark_row, rows_here]
        stay = more | (src + 1 >= sources)
        next_k = jnp.where(more, k + 1, jnp.where(stay, k, 0))
        return jnp.where(stay, src, src + 1), next_k

    def fetch(ref, page_ids):
        return jnp.concatenate([ref[p] for p in page_ids], axis=0)

    def scale_row(ref, page_ids):
        return by_page([jnp.broadcast_to(ref[p], (SUB, LANES)) for p in page_ids])

    def score_step(it, carry):
        top, at = carry
        for pair in range(ROUND // 2):
            ats = [at, advance(at)]
            at = advance(ats[1])
            info_of = [[page_of(one, i) for i in range(per_group)] for one in ats]
            ids = [[p for p, _ in one] for one in info_of]
            heads_of = [group_of(one) for one in ats]
            kk = jnp.concatenate([fetch(k_buf, one) for one in ids], axis=1)
            qa, qb = [q_all[owner] for owner, _, _ in heads_of]
            lhs = jnp.concatenate(
                [jnp.concatenate([qa, blank], axis=1), jnp.concatenate([blank, qb], axis=1)], axis=0
            )
            s = nt(lhs, kk)
            for x in range(2):
                g = it * ROUND + 2 * pair + x
                live_row = by_page([jnp.full((SUB, LANES), n, I32) for _, n in info_of[x]])
                is_live = token < live_row
                scale = scale_row(kse, ids[x])
                tiles = []
                for t in range(heads // SUB):
                    tile = s[x * heads + t * SUB : x * heads + (t + 1) * SUB] * scale
                    tiles.append(jnp.where(is_live & kv_masks[t], tile, FLOOR))
                tile = jnp.concatenate(tiles, axis=0)
                scores[g] = tile
                mine = jnp.broadcast_to(jnp.max(tile, axis=1, keepdims=True), (heads, LANES))
                top = jnp.maximum(top + (1.0 - heads_of[x][1]) * DROP, mine)
                peaks[g] = top
        return top, at

    first = (jnp.int32(0), jnp.int32(0))
    lax.fori_loop(0, steps, score_step, (jnp.full((heads, LANES), FLOOR, F32), first))
    for cp in v_loads:
        cp.wait()

    def value_step(it, carry):
        acc, den, at = carry
        for pair in range(ROUND // 2):
            ats = [at, advance(at)]
            at = advance(ats[1])
            ids = [[page_of(one, i)[0] for i in range(per_group)] for one in ats]
            heads_of = [group_of(one) for one in ats]
            vv = jnp.concatenate([fetch(v_buf, one) for one in ids], axis=1)
            lhs, weights = [], []
            for x in range(2):
                g = it * ROUND + 2 * pair + x
                last = g - ats[x][1] + heads_of[x][2]
                weight = jnp.exp(scores[g] - peaks[last])
                scale = scale_row(vse, ids[x])
                scaled = [weight[t * SUB : (t + 1) * SUB] * scale for t in range(heads // SUB)]
                lhs.append(jnp.concatenate(scaled, axis=0).astype(BF16))
                weights.append(weight)
            o = nn(jnp.concatenate(lhs, axis=0), vv)
            for x in range(2):
                g = it * ROUND + 2 * pair + x
                keep = heads_of[x][1]
                acc = acc * keep + o[x * heads : (x + 1) * heads, x * dim : (x + 1) * dim]
                den = den * keep + weights[x]
                accs[g] = acc
                dens[g] = den
        return acc, den, at

    zero = jnp.zeros((heads, LANES), F32)
    lax.fori_loop(0, steps, value_step, (zero, zero, first))

    lane16 = iota((heads, LANES), 1)

    def outgoing(dest, num_at, lse_at):
        lse_tile = jnp.full((heads, LANES), FLOOR, F32)
        base = jnp.int32(0)
        for src in range(sources):
            base = base + jnp.where(src < dest, info[src, mark_row, rows_here], 0)
        for r in range(rows_here):
            mark = info[dest, mark_row, r]
            last = base + mark // 2
            some = (mark & 1).astype(F32)
            den = jnp.broadcast_to(jnp.sum(dens[last], axis=1, keepdims=True), (heads, LANES))
            den = jnp.maximum(den, 0.5)
            num_at[r] = (accs[last] * (some / den)).astype(BF16)
            lse = (peaks[last] + jnp.log(den)) * some + (some - 1.0) * (-FLOOR)
            lse_tile = jnp.where(lane16 == r, lse, lse_tile)
        lse_at[...] = lse_tile

    def num_copy(peer, owner):
        return pltpu.make_async_remote_copy(
            src_ref=num_send.at[peer],
            dst_ref=num_recv.at[owner],
            send_sem=n_send.at[peer],
            recv_sem=n_recv.at[owner],
            device_id={"req": peer},
            device_id_type=MESH,
        )

    def lse_copy(peer, owner):
        return pltpu.make_async_remote_copy(
            src_ref=lse_send.at[peer],
            dst_ref=lse_recv.at[owner],
            send_sem=l_send.at[peer],
            recv_sem=l_recv.at[owner],
            device_id={"req": peer},
            device_id_type=MESH,
        )

    def send_block(k, carry):
        peer = lax.rem(me + k, sources)
        outgoing(peer, num_send.at[peer], lse_send.at[peer])
        num_copy(peer, me).start()
        lse_copy(peer, me).start()
        return carry

    lax.fori_loop(1, sources, send_block, 0)
    outgoing(me, num_recv.at[me], lse_recv.at[me])
    for k in range(1, sources):
        peer = lax.rem(me + k, sources)
        lse_copy(peer, peer).wait_recv()
    for k in range(1, sources):
        peer = lax.rem(me + k, sources)
        num_copy(peer, peer).wait_recv()

    lses = [lse_recv[s] for s in range(sources)]
    top = functools.reduce(jnp.maximum, lses)
    shares = [jnp.exp(x - top) for x in lses]
    total = functools.reduce(jnp.add, shares)
    shares = [x / total for x in shares]
    for r in range(rows_here):
        got = jnp.zeros((heads, dim), F32)
        for s in range(sources):
            share = jnp.broadcast_to(shares[s][:, r : r + 1], (heads, dim))
            got = got + share * num_recv[s, r].astype(F32)
        mixed[r * heads : (r + 1) * heads, :] = got
    for h in range(heads):
        rows = mixed[pl.ds(h, rows_here, stride=heads), :]
        att_all[me, :, h * dim : (h + 1) * dim] = rows.astype(BF16)

    def att_copy(peer, owner):
        return pltpu.make_async_remote_copy(
            src_ref=att_all.at[owner],
            dst_ref=att_all.at[owner],
            send_sem=a_send.at[peer],
            recv_sem=a_recv.at[owner],
            device_id={"req": peer},
            device_id_type=MESH,
        )

    for k in range(1, sources):
        att_copy(lax.rem(me + k, sources), me).start()
    for cp in w_loads:
        cp.wait()
    for k in range(1, sources):
        peer = lax.rem(me + k, sources)
        att_copy(peer, peer).wait_recv()

    att = att_all[...].reshape(requests, width)
    cols = w_buf.shape[1] // nz

    def term_copy(peer, owner):
        return pltpu.make_async_remote_copy(
            src_ref=term_send.at[peer],
            dst_ref=term_recv.at[owner],
            send_sem=z_send.at[peer],
            recv_sem=z_recv.at[owner],
            device_id={"head": peer},
            device_id_type=MESH,
        )

    def project(z):
        return nn(att, w_buf[:, pl.ds(pl.multiple_of(z * cols, cols), cols)])

    if cols % LANES == 0:
        for k in range(1, nz):
            peer = lax.rem(mz + k, nz)
            term_send[peer] = project(peer).astype(BF16)
            term_copy(peer, mz).start()
        result = project(mz)
    else:
        every = nn(att, w_buf[...])
        for z in range(nz):
            term_send[z] = every[:, z * cols : (z + 1) * cols].astype(BF16)
        for k in range(1, nz):
            term_copy(lax.rem(mz + k, nz), mz).start()
        result = term_send[mz].astype(F32)
    for k in range(1, nz):
        peer = lax.rem(mz + k, nz)
        term_copy(peer, peer).wait_recv()
        result = result + term_recv[peer].astype(F32)
    out_ref[...] = result.astype(BF16)

    for k in range(1, sources):
        peer = lax.rem(me + k, sources)
        info_copy(peer, me).wait_send()
        q_copy(k, me).wait_send()
        num_copy(peer, me).wait_send()
        lse_copy(peer, me).wait_send()
        att_copy(peer, me).wait_send()
    for k in range(1, nz):
        term_copy(lax.rem(mz + k, nz), mz).wait_send()


def on_device(
    queries,
    k_codes,
    value_quantized_codes,
    key_page_scale,
    value_page_scale,
    lengths,
    page_table,
    out_weight,
):
    pages, page_size, kv_local, dim = k_codes.shape
    rows_here, heads, _ = queries.shape
    sources, nz = lax.axis_size("req"), lax.axis_size("head")
    requests = rows_here * sources
    page_rows = page_size * kv_local
    per_group = LANES // page_rows
    group_bound = (pages + (per_group - 1) * requests) // per_group + sources
    n_groups = -(-group_bound // ROUND) * ROUND
    list_bound = (pages + (per_group - 1) * rows_here) // per_group
    slot_rows = -(-list_bound * per_group // LANES)
    group_rows = -(-list_bound // LANES)
    info_rows = -(-(slot_rows + group_rows + 1) // SUB) * SUB
    k_rows = k_codes.reshape(pages, page_rows, dim)
    v_rows = value_quantized_codes.reshape(pages, page_rows, dim)
    width = heads * dim
    columns = out_weight.shape[1]
    cfg = dict(
        sources=sources,
        nz=nz,
        rows_here=rows_here,
        heads=heads,
        dim=dim,
        pages=pages,
        page_rows=page_rows,
        page_size=page_size,
        n_groups=n_groups,
        per_group=per_group,
        slot_rows=slot_rows,
        group_rows=group_rows,
    )
    vmem = pl.BlockSpec(memory_space=pltpu.VMEM)
    smem = pl.BlockSpec(memory_space=pltpu.SMEM)
    hbm = pl.BlockSpec(memory_space=pl.ANY)
    dma = pltpu.SemaphoreType.DMA
    info = pl.pallas_call(
        functools.partial(list_kernel, cfg),
        out_shape=jax.ShapeDtypeStruct((sources, info_rows, LANES), I32),
        in_specs=[smem, vmem],
        out_specs=vmem,
        name="lists",
    )(lengths, page_table)
    return pl.pallas_call(
        functools.partial(kernel, cfg),
        out_shape=jax.ShapeDtypeStruct((requests, columns // nz), BF16),
        in_specs=[vmem, vmem, vmem, hbm, hbm, hbm, hbm],
        out_specs=vmem,
        scratch_shapes=[
            pltpu.VMEM(info.shape, I32),
            pltpu.SMEM(info.shape, I32),
            pltpu.VMEM((requests, heads, dim), BF16),
            pltpu.VMEM(k_rows.shape, BF16),
            pltpu.VMEM(v_rows.shape, BF16),
            pltpu.VMEM(out_weight.shape, BF16),
            pltpu.VMEM((pages, 1, LANES), F32),
            pltpu.VMEM((pages, 1, LANES), F32),
            pltpu.VMEM((n_groups, heads, LANES), F32),
            pltpu.VMEM((n_groups, heads, LANES), F32),
            pltpu.VMEM((n_groups, heads, LANES), F32),
            pltpu.VMEM((n_groups, heads, LANES), F32),
            pltpu.VMEM((sources, rows_here, heads, dim), BF16),
            pltpu.VMEM((sources, heads, LANES), F32),
            pltpu.VMEM((sources, rows_here, heads, dim), BF16),
            pltpu.VMEM((sources, heads, LANES), F32),
            pltpu.VMEM((rows_here * heads, dim), F32),
            pltpu.VMEM((sources, rows_here, width), BF16),
            pltpu.VMEM((nz, requests, columns // nz), BF16),
            pltpu.VMEM((nz, requests, columns // nz), BF16),
            dma,
            dma((3, 4)),
            dma,
            dma,
            dma((sources,)),
            dma((sources,)),
            dma((sources,)),
            dma((sources,)),
            dma((sources,)),
            dma((sources,)),
            dma((sources,)),
            dma((sources,)),
            dma((sources,)),
            dma((sources,)),
            dma((nz,)),
            dma((nz,)),
        ],
        compiler_params=pltpu.CompilerParams(
            vmem_limit_bytes=62 * 1024 * 1024, collective_id=0, has_side_effects=True
        ),
        name="paged",
    )(
        info,
        key_page_scale.T,
        value_page_scale.T,
        queries,
        k_rows,
        v_rows,
        out_weight,
    )


def solution(mesh):
    in_specs = (
        P("req", "head", None),
        P("req", None, "head", None),
        P("req", None, "head", None),
        P("req", "head"),
        P("req", "head"),
        P("req"),
        P("req", None),
        P("head", "req"),
    )
    out_specs = P(None, ("req", "head"))
    return jax.shard_map(
        on_device, mesh=mesh, in_specs=in_specs, out_specs=out_specs, check_vma=False
    )
```

time: 157 us -> 81.1 us (0.52)
  blocking collectives: 51.5 us -> 0 us
  Pallas kernels: 34.4 us -> 79.3 us
  local copies, waits for them, and re-layouts: 28.6 us -> 1.47 us
  waiting for transfers between devices: 20.4 us -> 0 us
  between operations: 14.2 us -> 0.01 us
  other arithmetic: 3.99 us -> 0 us
  matrix products: 3.64 us -> 0 us
    pallas_call x2, Pallas kernels: 34.4 us -> 79.3 us  [the longest x1 77.1 us: on_device(): pl.pallas_call(functools.partial(kernel, cfg), out_shape=jax.ShapeDtypeSt...]
    all_gather x3 -> x0, blocking collectives: 30.3 us -> none  [the longest x1 10.9 us: on_device(): table = lax.all_gather(page_table, 'req', axis=0, tiled=True)]
    reduce_scatter x1 -> x0, waiting for transfers between devices: 20.4 us -> none  [on_device(): lax.psum_scatter(terms.astype(jnp.bfloat16), 'head', scatter_dimension=1,...]
    reshape x2 -> x0, local copies, waits for them, and re-layouts: 14.9 us -> none  [the longest x1 7.48 us: on_device(): scale = scale.reshape(pages // GROUP, group_rows)]
    all_to_all x1 -> x0, blocking collectives: 13.5 us -> none  [on_device(): lax.all_to_all(partial_sums.reshape(sources, rows_here, width + LANES), '...]
    broadcast_in_dim x2 -> x0, local copies, waits for them, and re-layouts: 9.65 us -> none  [the longest x1 5.89 us: on_device(): jnp.broadcast_to(token < live[:, None, None], full)]
    unnamed x1 -> x0, blocking collectives: 7.68 us -> none
    dot_general x1 -> x0, matrix products: 3.64 us -> none  [on_device(): jnp.dot(lax.all_gather(attention.astype(jnp.bfloat16), 'req', axis=0, til...]
  transfers between devices with their start and end apart: 1 -> 0, of which waited for: 1 -> 0; matrix products, arithmetic and copies ran while one was open for 0% -> 0% of each run, Pallas kernels for 0% -> 0%
where the time goes in v1:
time: 81.1 us; the launch traced here: 80.8 us
  Pallas kernels  79.3 us (98%)
  local copies, waits for them, and re-layouts  1.47 us (2%)
    pallas_call x1, Pallas kernels, on_device(): pl.pallas_call(functools.partial(kernel, cfg), out_shape=jax.ShapeDtypeSt...  77.1 us
    pallas_call x1, Pallas kernels, on_device(): pl.pallas_call(functools.partial(list_kernel, cfg), out_shape=jax.ShapeDt...  2.26 us

profile of v1, /device:TPU:0, one launch (start us, length us, event | category | flops | bytes accessed | tf_op | source)
XLA Modules:
  0.0 80.8 jit_solution(1576773479474007555)
XLA Ops:
  0.0 2.3 %lists.1.info_ref = s32[8,16,128]{2,1,0:T(8,128)} custom-call(s32[16]{0:T(128)} %lengths_ref.1, s32[16,128]{1,0:T(8,128)} %table_ref.1), custom_call_target="tpu_custom_call" | custom-call | tf_op jit(solution)/shard_map/lists/pallas_call | solution.py:522
  2.3 77.1 %paged.1 = bf16[128,256]{1,0:T(8,128)(2,1)} custom-call(s32[8,16,128]{2,1,0:T(8,128)} %lists.1.info_ref, f32[2,1024]{1,0:T(2,128)} %bitcast.6, f32[2,1024]{1,0:T(2,128)} %bitcast.7, bf16[16,16,128]{2,1,0:T(8,128)(2,1)} %q_hbm.1, bf16[1024,32,128]{2,1,0:T(8,128)(2,1)} %bitcast.4, bf16[1024,32,128]{2,1,0:T(8,128)(2,1)} %bitcast.5, bf16[2048,1024]{1,0:T(8,128)(2,1)} %w_hbm.1), custom_call_target="tpu_custom_call" | custom-call | tf_op jit(solution)/shard_map/paged/pallas_call | solution.py:529
  79.3 1.5 %copy.10 = bf16[128,256]{1,0:T(8,128)(2,1)} copy(bf16[128,256]{1,0:T(8,128)(2,1)} %paged.1) | data formatting | bytes 131072

commit v2 on v1

--- a/solution.py
+++ b/solution.py
@@ -15,6 +15,7 @@
 SUB = 8
 LIVE_BITS = 5
 ROUND = 8
+FIELDS = 16
 F32 = jnp.float32
 BF16 = jnp.bfloat16
 I32 = jnp.int32
@@ -116,17 +117,24 @@
     w_hbm,
     out_ref,
     info_all,
-    info,
+    table_vmem,
+    table,
+    flat,
     q_all,
     k_buf,
     v_buf,
     w_buf,
     kse,
     vse,
+    bias,
     scores,
     peaks,
     dens,
     accs,
+    pair_send,
+    pair_lse_send,
+    pair_recv,
+    pair_lse_recv,
     num_send,
     lse_send,
     num_recv,
@@ -143,12 +151,18 @@
     t_recv,
     q_send,
     q_recv,
+    q_pass,
+    p_send,
+    p_recv,
+    pl_send,
+    pl_recv,
     n_send,
     n_recv,
     l_send,
     l_recv,
     a_send,
     a_recv,
+    a_pass,
     z_send,
     z_recv,
 ):
@@ -163,7 +177,18 @@
     width = heads * dim
     me = lax.axis_index("req")
     mz = lax.axis_index("head")
+    chips = sources // 2
+    chip, core = me // 2, lax.rem(me, 2)
+    partner = me + 1 - 2 * core
+
+    def other_chip(k):
+        return lax.rem(chip + k, chips)
+
+    far = range(chips - 1, 0, -1)
     slot_rows, mark_row = cfg["slot_rows"], cfg["slot_rows"] + cfg["group_rows"]
+    last_row = mark_row + cfg["group_rows"]
+    per_row = LANES // per_group
+    per_row_bits = int(math.log2(per_row))
 
     q_load = pltpu.make_async_copy(q_hbm, q_all.at[pl.ds(me * rows_here, rows_here)], q_sem)
     q_load.start()
@@ -199,23 +224,56 @@
             device_id_type=MESH,
         )
 
-    def q_copy(k, owner):
-        peer = lax.rem(me + k, sources)
-        rows = pl.ds(owner * rows_here, rows_here)
+    def remote(src, dst, send, recv, **where):
         return pltpu.make_async_remote_copy(
-            src_ref=q_all.at[rows],
-            dst_ref=q_all.at[rows],
-            send_sem=q_send.at[peer],
-            recv_sem=q_recv.at[owner],
-            device_id={"req": peer},
+            src_ref=src,
+            dst_ref=dst,
+            send_sem=send,
+            recv_sem=recv,
+            device_id=where,
             device_id_type=MESH,
         )
 
-    for k in range(1, sources):
+    def gather(rows_of, send, recv, passing):
+        def direct(peer, owner):
+            return remote(rows_of(owner), rows_of(owner), send.at[peer], recv.at[owner], req=peer)
+
+        def onward(owner):
+            return remote(rows_of(owner), rows_of(owner), passing.at[owner], recv.at[owner], req=partner)
+
+        def begin():
+            for k in far:
+                direct(other_chip(k) * 2 + core, me).start()
+            direct(partner, me).start()
+
+        def relay():
+            for k in far:
+                owner = other_chip(k) * 2 + core
+                direct(owner, owner).wait_recv()
+                onward(owner).start()
+
+        def arrive():
+            direct(partner, partner).wait_recv()
+            for k in far:
+                owner = other_chip(k) * 2 + 1 - core
+                onward(owner).wait_recv()
+
+        def finish():
+            direct(partner, me).wait_send()
+            for k in far:
+                owner = other_chip(k) * 2 + core
+                direct(owner, me).wait_send()
+                onward(owner).wait_send()
+
+        return begin, relay, arrive, finish
+
+    q_begin, q_relay, q_arrive, q_finish = gather(
+        lambda owner: q_all.at[pl.ds(owner * rows_here, rows_here)], q_send, q_recv, q_pass
+    )
+    for k in range(sources - 1, 0, -1):
         info_copy(lax.rem(me + k, sources), me).start()
     q_load.wait()
-    for k in range(1, sources):
-        q_copy(k, me).start()
+    q_begin()
 
     lane_sub = iota((LANES, LANES), 0)
     for src, dst, factor in ((kscale_ref, kse, 1.0 / math.sqrt(dim)), (vscale_ref, vse, 1.0)):
@@ -231,11 +289,51 @@
     for k in range(1, sources):
         peer = lax.rem(me + k, sources)
         info_copy(peer, peer).wait_recv()
-    to_smem = pltpu.make_async_copy(info_all, info, smem_sem)
+    for src in range(sources):
+        raw = info_all[src]
+        value = raw[slot_rows:mark_row]
+        table_vmem[src, :slot_rows, :] = raw[:slot_rows] >> LIVE_BITS
+        table_vmem[src, slot_rows:mark_row, :] = (value & (rows_here - 1)) + src * rows_here
+        table_vmem[src, mark_row : 2 * mark_row - slot_rows, :] = value >> int(math.log2(rows_here))
+        table_vmem[src, last_row : last_row + 1, :] = raw[mark_row : mark_row + 1]
+    to_smem = pltpu.make_async_copy(table_vmem, table, smem_sem)
     to_smem.start()
     to_smem.wait()
-    for k in range(1, sources):
-        q_copy(k, lax.rem(me + k, sources)).wait_recv()
+
+    def flatten(it, at):
+        src, k = at
+        for j in range(ROUND):
+            block = k >> per_row_bits
+            column = (k & (per_row - 1)) * per_group
+            for i in range(per_group):
+                flat[it, j * FIELDS + i] = table[src, block, column + i]
+            row, column = k >> 7, k & (LANES - 1)
+            flat[it, j * FIELDS + 4] = table[src, slot_rows + row, column]
+            last = table[src, mark_row + row, column]
+            flat[it, j * FIELDS + 5] = it * ROUND + j - k + (last >> 1)
+            flat[it, j * FIELDS + 6] = last & 1
+            flat[it, j * FIELDS + 7] = src * (slot_rows * per_row) + k
+            more = k + 1 < table[src, last_row, rows_here]
+            stay = more | (src + 1 >= sources)
+            k = jnp.where(more, k + 1, jnp.where(stay, k, 0))
+            src = jnp.where(stay, src, src + 1)
+        return src, k
+
+    lax.fori_loop(0, steps, flatten, (jnp.int32(0), jnp.int32(0)))
+
+    spread = jnp.where(iota((LANES, LANES), 0) % per_group == iota((LANES, LANES), 1) // page_rows, 1.0, 0.0)
+    spread = spread.astype(BF16)
+    chosen = iota((per_row, LANES), 1) // per_group == iota((per_row, LANES), 0)
+    token_row = ((iota((1, LANES), 1) % page_rows) // kv_local).astype(F32)
+    for src in range(sources):
+        live = (info_all[src] & ((1 << LIVE_BITS) - 1)).astype(F32)
+        picks = [jnp.where(chosen, live[b : b + 1], 0.0) for b in range(slot_rows)]
+        wide = nn(jnp.concatenate(picks, axis=0).astype(BF16), spread)
+        rows = slice(src * slot_rows * per_row, (src + 1) * slot_rows * per_row)
+        bias[rows, 0, :] = jnp.where(token_row < wide, 0.0, FLOOR)
+
+    q_relay()
+    q_arrive()
     for cp in k_loads:
         cp.wait()
 
@@ -251,159 +349,161 @@
             got = jnp.where(lane8 < (i + 1) * page_rows, parts[i], got)
         return got
 
-    def page_of(at, i):
-        src, k = at
-        lane_at = (k & (LANES // per_group - 1)) * per_group
-        value = info[src, k // (LANES // per_group), lane_at + i]
-        return value >> LIVE_BITS, value & ((1 << LIVE_BITS) - 1)
-
-    def group_of(at):
-        src, k = at
-        value = info[src, slot_rows + k // LANES, k & (LANES - 1)]
-        owner = src * rows_here + (value & (rows_here - 1))
-        rest = value // rows_here
-        return owner, (rest & 1).astype(F32), rest // 2
-
-    def advance(at):
-        src, k = at
-        more = k + 1 < info[src, mark_row, rows_here]
-        stay = more | (src + 1 >= sources)
-        next_k = jnp.where(more, k + 1, jnp.where(stay, k, 0))
-        return jnp.where(stay, src, src + 1), next_k
-
     def fetch(ref, page_ids):
         return jnp.concatenate([ref[p] for p in page_ids], axis=0)
 
     def scale_row(ref, page_ids):
         return by_page([jnp.broadcast_to(ref[p], (SUB, LANES)) for p in page_ids])
 
-    def score_step(it, carry):
-        top, at = carry
+    def same_owner(it, j):
+        return jnp.full((heads, LANES), flat[it, j * FIELDS + 6], I32) > 0
+
+    def score_step(it, top):
         for pair in range(ROUND // 2):
-            ats = [at, advance(at)]
-            at = advance(ats[1])
-            info_of = [[page_of(one, i) for i in range(per_group)] for one in ats]
-            ids = [[p for p, _ in one] for one in info_of]
-            heads_of = [group_of(one) for one in ats]
+            js = (2 * pair, 2 * pair + 1)
+            ids = [[flat[it, j * FIELDS + i] for i in range(per_group)] for j in js]
             kk = jnp.concatenate([fetch(k_buf, one) for one in ids], axis=1)
-            qa, qb = [q_all[owner] for owner, _, _ in heads_of]
+            qa, qb = [q_all[flat[it, j * FIELDS + 4]] for j in js]
             lhs = jnp.concatenate(
                 [jnp.concatenate([qa, blank], axis=1), jnp.concatenate([blank, qb], axis=1)], axis=0
             )
             s = nt(lhs, kk)
-            for x in range(2):
-                g = it * ROUND + 2 * pair + x
-                live_row = by_page([jnp.full((SUB, LANES), n, I32) for _, n in info_of[x]])
-                is_live = token < live_row
+            for x, j in enumerate(js):
+                g = it * ROUND + j
                 scale = scale_row(kse, ids[x])
+                shift = jnp.broadcast_to(bias[flat[it, j * FIELDS + 7]], (SUB, LANES))
                 tiles = []
                 for t in range(heads // SUB):
-                    tile = s[x * heads + t * SUB : x * heads + (t + 1) * SUB] * scale
-                    tiles.append(jnp.where(is_live & kv_masks[t], tile, FLOOR))
+                    tile = s[x * heads + t * SUB : x * heads + (t + 1) * SUB] * scale + shift
+                    tiles.append(jnp.where(kv_masks[t], tile, FLOOR))
                 tile = jnp.concatenate(tiles, axis=0)
                 scores[g] = tile
                 mine = jnp.broadcast_to(jnp.max(tile, axis=1, keepdims=True), (heads, LANES))
-                top = jnp.maximum(top + (1.0 - heads_of[x][1]) * DROP, mine)
+                top = jnp.where(same_owner(it, j), jnp.maximum(top, mine), mine)
                 peaks[g] = top
-        return top, at
-
-    first = (jnp.int32(0), jnp.int32(0))
-    lax.fori_loop(0, steps, score_step, (jnp.full((heads, LANES), FLOOR, F32), first))
+        return top
+
+    lax.fori_loop(0, steps, score_step, jnp.full((heads, LANES), FLOOR, F32))
     for cp in v_loads:
         cp.wait()
 
     def value_step(it, carry):
-        acc, den, at = carry
+        acc, den = carry
         for pair in range(ROUND // 2):
-            ats = [at, advance(at)]
-            at = advance(ats[1])
-            ids = [[page_of(one, i)[0] for i in range(per_group)] for one in ats]
-            heads_of = [group_of(one) for one in ats]
+            js = (2 * pair, 2 * pair + 1)
+            ids = [[flat[it, j * FIELDS + i] for i in range(per_group)] for j in js]
             vv = jnp.concatenate([fetch(v_buf, one) for one in ids], axis=1)
             lhs, weights = [], []
-            for x in range(2):
-                g = it * ROUND + 2 * pair + x
-                last = g - ats[x][1] + heads_of[x][2]
-                weight = jnp.exp(scores[g] - peaks[last])
+            for x, j in enumerate(js):
+                weight = jnp.exp(scores[it * ROUND + j] - peaks[flat[it, j * FIELDS + 5]])
                 scale = scale_row(vse, ids[x])
                 scaled = [weight[t * SUB : (t + 1) * SUB] * scale for t in range(heads // SUB)]
                 lhs.append(jnp.concatenate(scaled, axis=0).astype(BF16))
                 weights.append(weight)
             o = nn(jnp.concatenate(lhs, axis=0), vv)
-            for x in range(2):
-                g = it * ROUND + 2 * pair + x
-                keep = heads_of[x][1]
-                acc = acc * keep + o[x * heads : (x + 1) * heads, x * dim : (x + 1) * dim]
-                den = den * keep + weights[x]
+            for x, j in enumerate(js):
+                g = it * ROUND + j
+                keep = same_owner(it, j)
+                mine = o[x * heads : (x + 1) * heads, x * dim : (x + 1) * dim]
+                acc = jnp.where(keep, acc + mine, mine)
+                den = jnp.where(keep, den + weights[x], weights[x])
                 accs[g] = acc
                 dens[g] = den
-        return acc, den, at
+        return acc, den
 
     zero = jnp.zeros((heads, LANES), F32)
-    lax.fori_loop(0, steps, value_step, (zero, zero, first))
+    lax.fori_loop(0, steps, value_step, (zero, zero))
 
     lane16 = iota((heads, LANES), 1)
 
-    def outgoing(dest, num_at, lse_at):
-        lse_tile = jnp.full((heads, LANES), FLOOR, F32)
+    def first_group(dest):
         base = jnp.int32(0)
         for src in range(sources):
-            base = base + jnp.where(src < dest, info[src, mark_row, rows_here], 0)
+            base = base + jnp.where(src < dest, table[src, last_row, rows_here], 0)
+        return base
+
+    def local_part(dest, base, r):
+        mark = table[dest, last_row, r]
+        last = base + (mark >> 1)
+        some = (mark & 1).astype(F32)
+        den = jnp.broadcast_to(jnp.sum(dens[last], axis=1, keepdims=True), (heads, LANES))
+        den = jnp.maximum(den, 0.5)
+        num = accs[last] * (some / den)
+        return num, (peaks[last] + jnp.log(den)) * some + (some - 1.0) * (-FLOOR)
+
+    def pair_copy(c):
+        return remote(pair_send.at[c], pair_recv.at[c], p_send.at[c], p_recv.at[c], req=partner)
+
+    def pair_lse_copy(c):
+        return remote(pair_lse_send.at[c], pair_lse_recv.at[c], pl_send.at[c], pl_recv.at[c], req=partner)
+
+    def num_copy(to, owner):
+        return remote(
+            num_send.at[to], num_recv.at[owner], n_send.at[to], n_recv.at[owner], req=to * 2 + core
+        )
+
+    def lse_copy(to, owner):
+        return remote(
+            lse_send.at[to], lse_recv.at[owner], l_send.at[to], l_recv.at[owner], req=to * 2 + core
+        )
+
+    def for_partner(k, carry):
+        c = other_chip(chips - 1 - k)
+        dest = c * 2 + 1 - core
+        base = first_group(dest)
+        tile = jnp.full((heads, LANES), FLOOR, F32)
         for r in range(rows_here):
-            mark = info[dest, mark_row, r]
-            last = base + mark // 2
-            some = (mark & 1).astype(F32)
-            den = jnp.broadcast_to(jnp.sum(dens[last], axis=1, keepdims=True), (heads, LANES))
-            den = jnp.maximum(den, 0.5)
-            num_at[r] = (accs[last] * (some / den)).astype(BF16)
-            lse = (peaks[last] + jnp.log(den)) * some + (some - 1.0) * (-FLOOR)
-            lse_tile = jnp.where(lane16 == r, lse, lse_tile)
-        lse_at[...] = lse_tile
-
-    def num_copy(peer, owner):
-        return pltpu.make_async_remote_copy(
-            src_ref=num_send.at[peer],
-            dst_ref=num_recv.at[owner],
-            send_sem=n_send.at[peer],
-            recv_sem=n_recv.at[owner],
-            device_id={"req": peer},
-            device_id_type=MESH,
-        )
-
-    def lse_copy(peer, owner):
-        return pltpu.make_async_remote_copy(
-            src_ref=lse_send.at[peer],
-            dst_ref=lse_recv.at[owner],
-            send_sem=l_send.at[peer],
-            recv_sem=l_recv.at[owner],
-            device_id={"req": peer},
-            device_id_type=MESH,
-        )
+            num, lse = local_part(dest, base, r)
+            pair_send[c, r] = num.astype(BF16)
+            tile = jnp.where(lane16 == r, lse, tile)
+        pair_lse_send[c] = tile
+        pair_copy(c).start()
+        pair_lse_copy(c).start()
+        return carry
+
+    lax.fori_loop(0, chips, for_partner, 0)
+
+    def merge(c, num_at, lse_at):
+        dest = c * 2 + core
+        base = first_group(dest)
+        theirs = pair_lse_recv[c]
+        tile = jnp.full((heads, LANES), FLOOR, F32)
+        for r in range(rows_here):
+            num, lse = local_part(dest, base, r)
+            their = jnp.broadcast_to(theirs[:, r : r + 1], (heads, LANES))
+            high = jnp.maximum(lse, their)
+            a, b = jnp.exp(lse - high), jnp.exp(their - high)
+            total = a + b
+            got = (num * a + pair_recv[c, r].astype(F32) * b) / total
+            num_at[r] = got.astype(BF16)
+            tile = jnp.where(lane16 == r, high + jnp.log(total), tile)
+        lse_at[...] = tile
 
     def send_block(k, carry):
-        peer = lax.rem(me + k, sources)
-        outgoing(peer, num_send.at[peer], lse_send.at[peer])
-        num_copy(peer, me).start()
-        lse_copy(peer, me).start()
+        c = other_chip(chips - 1 - k)
+        merge(c, num_send.at[c], lse_send.at[c])
+        num_copy(c, chip).start()
+        lse_copy(c, chip).start()
         return carry
 
-    lax.fori_loop(1, sources, send_block, 0)
-    outgoing(me, num_recv.at[me], lse_recv.at[me])
-    for k in range(1, sources):
-        peer = lax.rem(me + k, sources)
-        lse_copy(peer, peer).wait_recv()
-    for k in range(1, sources):
-        peer = lax.rem(me + k, sources)
-        num_copy(peer, peer).wait_recv()
-
-    lses = [lse_recv[s] for s in range(sources)]
+    for k in range(chips - 1, -1, -1):
+        pair_lse_copy(other_chip(k)).wait_recv()
+        pair_copy(other_chip(k)).wait_recv()
+    lax.fori_loop(0, chips - 1, send_block, 0)
+    merge(chip, num_recv.at[chip], lse_recv.at[chip])
+    for k in far:
+        c = other_chip(k)
+        lse_copy(c, c).wait_recv()
+        num_copy(c, c).wait_recv()
+
+    lses = [lse_recv[s] for s in range(chips)]
     top = functools.reduce(jnp.maximum, lses)
     shares = [jnp.exp(x - top) for x in lses]
     total = functools.reduce(jnp.add, shares)
     shares = [x / total for x in shares]
     for r in range(rows_here):
         got = jnp.zeros((heads, dim), F32)
-        for s in range(sources):
+        for s in range(chips):
             share = jnp.broadcast_to(shares[s][:, r : r + 1], (heads, dim))
             got = got + share * num_recv[s, r].astype(F32)
         mixed[r * heads : (r + 1) * heads, :] = got
@@ -411,23 +511,12 @@
         rows = mixed[pl.ds(h, rows_here, stride=heads), :]
         att_all[me, :, h * dim : (h + 1) * dim] = rows.astype(BF16)
 
-    def att_copy(peer, owner):
-        return pltpu.make_async_remote_copy(
-            src_ref=att_all.at[owner],
-            dst_ref=att_all.at[owner],
-            send_sem=a_send.at[peer],
-            recv_sem=a_recv.at[owner],
-            device_id={"req": peer},
-            device_id_type=MESH,
-        )
-
-    for k in range(1, sources):
-        att_copy(lax.rem(me + k, sources), me).start()
+    a_begin, a_relay, a_arrive, a_finish = gather(lambda owner: att_all.at[owner], a_send, a_recv, a_pass)
+    a_begin()
     for cp in w_loads:
         cp.wait()
-    for k in range(1, sources):
-        peer = lax.rem(me + k, sources)
-        att_copy(peer, peer).wait_recv()
+    a_relay()
+    a_arrive()
 
     att = att_all[...].reshape(requests, width)
     cols = w_buf.shape[1] // nz
@@ -467,10 +556,15 @@
     for k in range(1, sources):
         peer = lax.rem(me + k, sources)
         info_copy(peer, me).wait_send()
-        q_copy(k, me).wait_send()
-        num_copy(peer, me).wait_send()
-        lse_copy(peer, me).wait_send()
-        att_copy(peer, me).wait_send()
+    q_finish()
+    a_finish()
+    for c in range(chips):
+        pair_copy(c).wait_send()
+        pair_lse_copy(c).wait_send()
+    for k in far:
+        c = other_chip(k)
+        num_copy(c, chip).wait_send()
+        lse_copy(c, chip).wait_send()
     for k in range(1, nz):
         term_copy(lax.rem(mz + k, nz), mz).wait_send()
 
@@ -497,6 +591,8 @@
     slot_rows = -(-list_bound * per_group // LANES)
     group_rows = -(-list_bound // LANES)
     info_rows = -(-(slot_rows + group_rows + 1) // SUB) * SUB
+    table_rows = -(-(slot_rows + 2 * group_rows + 1) // SUB) * SUB
+    chips = sources // 2
     k_rows = k_codes.reshape(pages, page_rows, dim)
     v_rows = value_quantized_codes.reshape(pages, page_rows, dim)
     width = heads * dim
@@ -533,21 +629,28 @@
         out_specs=vmem,
         scratch_shapes=[
             pltpu.VMEM(info.shape, I32),
-            pltpu.SMEM(info.shape, I32),
+            pltpu.VMEM((sources, table_rows, LANES), I32),
+            pltpu.SMEM((sources, table_rows, LANES), I32),
+            pltpu.SMEM((n_groups // ROUND, LANES), I32),
             pltpu.VMEM((requests, heads, dim), BF16),
             pltpu.VMEM(k_rows.shape, BF16),
             pltpu.VMEM(v_rows.shape, BF16),
             pltpu.VMEM(out_weight.shape, BF16),
             pltpu.VMEM((pages, 1, LANES), F32),
             pltpu.VMEM((pages, 1, LANES), F32),
+            pltpu.VMEM((sources * slot_rows * (LANES // per_group), 1, LANES), F32),
             pltpu.VMEM((n_groups, heads, LANES), F32),
             pltpu.VMEM((n_groups, heads, LANES), F32),
             pltpu.VMEM((n_groups, heads, LANES), F32),
             pltpu.VMEM((n_groups, heads, LANES), F32),
-            pltpu.VMEM((sources, rows_here, heads, dim), BF16),
-            pltpu.VMEM((sources, heads, LANES), F32),
-            pltpu.VMEM((sources, rows_here, heads, dim), BF16),
-            pltpu.VMEM((sources, heads, LANES), F32),
+            pltpu.VMEM((chips, rows_here, heads, dim), BF16),
+            pltpu.VMEM((chips, heads, LANES), F32),
+            pltpu.VMEM((chips, rows_here, heads, dim), BF16),
+            pltpu.VMEM((chips, heads, LANES), F32),
+            pltpu.VMEM((chips, rows_here, heads, dim), BF16),
+            pltpu.VMEM((chips, heads, LANES), F32),
+            pltpu.VMEM((chips, rows_here, heads, dim), BF16),
+            pltpu.VMEM((chips, heads, LANES), F32),
             pltpu.VMEM((rows_here * heads, dim), F32),
             pltpu.VMEM((sources, rows_here, width), BF16),
             pltpu.VMEM((nz, requests, columns // nz), BF16),
@@ -561,8 +664,14 @@
             dma((sources,)),
             dma((sources,)),
             dma((sources,)),
-            dma((sources,)),
-            dma((sources,)),
+            dma((chips,)),
+            dma((chips,)),
+            dma((chips,)),
+            dma((chips,)),
+            dma((chips,)),
+            dma((chips,)),
+            dma((chips,)),
+            dma((chips,)),
             dma((sources,)),
             dma((sources,)),
             dma((sources,)),

time: 81.1 us -> 69 us (0.85)
  Pallas kernels: 79.3 us -> 67.3 us
    pallas_call x1, Pallas kernels: 77.1 us -> 65 us  [on_device(): pl.pallas_call(functools.partial(kernel, cfg), out_shape=jax.ShapeDtypeSt...]
where the time goes in v2:
time: 69 us; the launch traced here: 68.8 us
  Pallas kernels  67.3 us (98%)
  local copies, waits for them, and re-layouts  1.47 us (2%)
    pallas_call x1, Pallas kernels, on_device(): pl.pallas_call(functools.partial(kernel, cfg), out_shape=jax.ShapeDtypeSt...  65 us
    pallas_call x1, Pallas kernels, on_device(): pl.pallas_call(functools.partial(list_kernel, cfg), out_shape=jax.ShapeDt...  2.26 us
    unnamed x1, local copies, waits for them, and re-layouts  1.47 us

profile of v2, /device:TPU:0, one launch (start us, length us, event | category | flops | bytes accessed | tf_op | source)
XLA Modules:
  0.0 68.8 jit_solution(3233817432927752244)
XLA Ops:
  0.0 2.3 %lists.1.info_ref = s32[8,16,128]{2,1,0:T(8,128)} custom-call(s32[16]{0:T(128)} %lengths_ref.1, s32[16,128]{1,0:T(8,128)} %table_ref.1), custom_call_target="tpu_custom_call" | custom-call | tf_op jit(solution)/shard_map/lists/pallas_call | solution.py:618
  2.3 65.0 %paged.1 = bf16[128,256]{1,0:T(8,128)(2,1)} custom-call(s32[8,16,128]{2,1,0:T(8,128)} %lists.1.info_ref, f32[2,1024]{1,0:T(2,128)} %bitcast.6, f32[2,1024]{1,0:T(2,128)} %bitcast.7, bf16[16,16,128]{2,1,0:T(8,128)(2,1)} %q_hbm.1, bf16[1024,32,128]{2,1,0:T(8,128)(2,1)} %bitcast.4, bf16[1024,32,128]{2,1,0:T(8,128)(2,1)} %bitcast.5, bf16[2048,1024]{1,0:T(8,128)(2,1)} %w_hbm.1), custom_call_target="tpu_custom_call" | custom-call | tf_op jit(solution)/shard_map/paged/pallas_call | solution.py:625
  67.3 1.5 %copy.10 = bf16[128,256]{1,0:T(8,128)(2,1)} copy(bf16[128,256]{1,0:T(8,128)(2,1)} %paged.1) | data formatting | bytes 131072

commit v3 on v2

--- a/solution.py
+++ b/solution.py
@@ -14,8 +14,9 @@
 LANES = 128
 SUB = 8
 LIVE_BITS = 5
-ROUND = 8
-FIELDS = 16
+OWNER_SHIFT = 7
+FIELDS = 8
+ROUND = LANES // FIELDS
 F32 = jnp.float32
 BF16 = jnp.bfloat16
 I32 = jnp.int32
@@ -36,7 +37,7 @@
 def list_kernel(cfg, lengths_ref, table_ref, out_ref):
     sources, rows_here, pages = cfg["sources"], cfg["rows_here"], cfg["pages"]
     page_size, per_group = cfg["page_size"], cfg["per_group"]
-    slot_rows, group_rows = cfg["slot_rows"], cfg["group_rows"]
+    list_rows = cfg["list_rows"]
     shape = (rows_here, LANES)
     row_id = iota(shape, 0)
     lengths = jnp.zeros(shape, I32)
@@ -59,51 +60,50 @@
     tri = jnp.where((i >= j) & (i // rows_here == j // rows_here), 1.0, 0.0).astype(BF16)
     ends = nn(tri, need.astype(BF16))
     starts = ends - need
-    slots = (starts * per_group + before).astype(I32)
-
-    key = jnp.full(shape, -1, I32)
-    page = jnp.zeros(shape, I32)
+    before, starts_int, need_int = before.astype(I32), starts.astype(I32), need.astype(I32)
+
+    high = jnp.full(shape, -1, I32)
+    low, lead, page, rest = high, high, high, high
     for d in range(sources):
-        slot = slots[d * rows_here : (d + 1) * rows_here] + d * (slot_rows * LANES)
-        key = jnp.where(mines[d], slot, key)
+        rows = slice(d * rows_here, (d + 1) * rows_here)
+        step = before[rows] >> 2
+        group = starts_int[rows] + step
+        column = (group & (ROUND - 1)) * FIELDS
+        place = before[rows] & 3
+        high = jnp.where(mines[d], d * list_rows + group // ROUND, high)
+        low = jnp.where(mines[d], column + place, low)
+        lead = jnp.where(mines[d] & (place == 0), column + per_group, lead)
         page = jnp.where(mines[d], locals_[d], page)
+        left = (need_int[rows] - 1 - step) * 2 + jnp.where(step == 0, 1, 0)
+        rest = jnp.where(mines[d], left, rest)
     one = (page >> 2).astype(F32)
     two = ((page & 3) * (1 << LIVE_BITS) + live).astype(F32)
-    high, low = key >> 7, key & (LANES - 1)
-    hi_rows = -(-(sources * slot_rows) // 16) * 16
+    rest = rest.astype(F32)
+    hi_rows = -(-(sources * list_rows) // 16) * 16
     hi_iota, lo_iota = iota((hi_rows, LANES), 0), iota((LANES, LANES), 0)
     lefts, rights = [], []
     for r in range(rows_here):
         row = slice(r, r + 1)
         lefts.append(jnp.where(hi_iota == high[row], 1.0, 0.0).astype(BF16))
-        same = lo_iota == low[row]
-        pair = [jnp.where(same, one[row], 0.0), jnp.where(same, two[row], 0.0)]
+        same, head = lo_iota == low[row], lo_iota == lead[row]
+        pair = [
+            jnp.where(same, one[row], jnp.where(head, float(r), 0.0)),
+            jnp.where(same, two[row], jnp.where(head, rest[row], 0.0)),
+        ]
         rights.append(jnp.concatenate(pair, axis=0).astype(BF16))
     found = nt(jnp.concatenate(lefts, axis=1), jnp.concatenate(rights, axis=1))
     found = (found[:, :LANES] * float(4 << LIVE_BITS) + found[:, LANES:]).astype(I32)
 
-    lane = iota(shape, 1).astype(F32)
     diag = row_id == iota(shape, 1)
     for d in range(sources):
         rows = slice(d * rows_here, (d + 1) * rows_here)
-        end, begin, some = ends[rows], starts[rows], need[rows] > 0.5
-        out_ref[d, :slot_rows, :] = found[d * slot_rows : (d + 1) * slot_rows]
-        for b in range(group_rows):
-            here = lane + float(b * LANES)
-            done = end <= here
-            owner = jnp.sum(jnp.where(done, 1.0, 0.0), axis=0, keepdims=True)
-            owner = jnp.minimum(owner, float(rows_here - 1))
-            last = jnp.min(jnp.where(done, 4096.0, end), axis=0, keepdims=True) - 1.0
-            opens = jnp.where((begin == here) & some, 1.0, 0.0)
-            opens = jnp.max(opens, axis=0, keepdims=True)
-            value = (last * 2.0 + (1.0 - opens)) * float(rows_here) + owner
-            out_ref[d, slot_rows + b : slot_rows + b + 1, :] = value.astype(I32)
+        end, some = ends[rows], need[rows] > 0.5
+        out_ref[d, :list_rows, :] = found[d * list_rows : (d + 1) * list_rows]
         mark = jnp.maximum(end - 1.0, 0.0) * 2.0 + jnp.where(some, 1.0, 0.0)
         mark = jnp.sum(jnp.where(diag, mark, 0.0), axis=0, keepdims=True)
-        size = jnp.maximum(jnp.max(end, axis=0, keepdims=True), 1.0)
+        size = jnp.max(end, axis=0, keepdims=True)
         mark = jnp.where(iota((1, LANES), 1) == rows_here, size, mark)
-        base = slot_rows + group_rows
-        out_ref[d, base : base + 1, :] = mark.astype(I32)
+        out_ref[d, list_rows : list_rows + 1, :] = mark.astype(I32)
 
 
 def kernel(
@@ -117,8 +117,9 @@
     w_hbm,
     out_ref,
     info_all,
-    table_vmem,
-    table,
+    mark_vmem,
+    marks,
+    flat_vmem,
     flat,
     q_all,
     k_buf,
@@ -146,7 +147,8 @@
     q_sem,
     load_sems,
     info_sem,
-    smem_sem,
+    mark_sem,
+    flat_sem,
     t_send,
     t_recv,
     q_send,
@@ -185,10 +187,8 @@
         return lax.rem(chip + k, chips)
 
     far = range(chips - 1, 0, -1)
-    slot_rows, mark_row = cfg["slot_rows"], cfg["slot_rows"] + cfg["group_rows"]
-    last_row = mark_row + cfg["group_rows"]
-    per_row = LANES // per_group
-    per_row_bits = int(math.log2(per_row))
+    list_rows = cfg["list_rows"]
+    flat_rows = flat_vmem.shape[0]
 
     q_load = pltpu.make_async_copy(q_hbm, q_all.at[pl.ds(me * rows_here, rows_here)], q_sem)
     q_load.start()
@@ -290,47 +290,47 @@
         peer = lax.rem(me + k, sources)
         info_copy(peer, peer).wait_recv()
     for src in range(sources):
-        raw = info_all[src]
-        value = raw[slot_rows:mark_row]
-        table_vmem[src, :slot_rows, :] = raw[:slot_rows] >> LIVE_BITS
-        table_vmem[src, slot_rows:mark_row, :] = (value & (rows_here - 1)) + src * rows_here
-        table_vmem[src, mark_row : 2 * mark_row - slot_rows, :] = value >> int(math.log2(rows_here))
-        table_vmem[src, last_row : last_row + 1, :] = raw[mark_row : mark_row + 1]
-    to_smem = pltpu.make_async_copy(table_vmem, table, smem_sem)
+        mark_vmem[src : src + 1, :] = info_all[src, list_rows : list_rows + 1, :]
+    to_smem = pltpu.make_async_copy(mark_vmem, marks, mark_sem)
     to_smem.start()
     to_smem.wait()
 
-    def flatten(it, at):
-        src, k = at
-        for j in range(ROUND):
-            block = k >> per_row_bits
-            column = (k & (per_row - 1)) * per_group
-            for i in range(per_group):
-                flat[it, j * FIELDS + i] = table[src, block, column + i]
-            row, column = k >> 7, k & (LANES - 1)
-            flat[it, j * FIELDS + 4] = table[src, slot_rows + row, column]
-            last = table[src, mark_row + row, column]
-            flat[it, j * FIELDS + 5] = it * ROUND + j - k + (last >> 1)
-            flat[it, j * FIELDS + 6] = last & 1
-            flat[it, j * FIELDS + 7] = src * (slot_rows * per_row) + k
-            more = k + 1 < table[src, last_row, rows_here]
-            stay = more | (src + 1 >= sources)
-            k = jnp.where(more, k + 1, jnp.where(stay, k, 0))
-            src = jnp.where(stay, src, src + 1)
-        return src, k
-
-    lax.fori_loop(0, steps, flatten, (jnp.int32(0), jnp.int32(0)))
-
-    spread = jnp.where(iota((LANES, LANES), 0) % per_group == iota((LANES, LANES), 1) // page_rows, 1.0, 0.0)
-    spread = spread.astype(BF16)
-    chosen = iota((per_row, LANES), 1) // per_group == iota((per_row, LANES), 0)
+    shape = (flat_rows, LANES)
+    lane, field = iota(shape, 1), iota(shape, 1) % FIELDS
+    group = iota(shape, 0) * ROUND + lane // FIELDS
+    joined = jnp.zeros(shape, I32)
+    base = jnp.int32(0)
+    for src in range(sources):
+        size = marks[src, rows_here]
+        rows = min(flat_rows, info_all.shape[1])
+        one = info_all[src, :rows, :]
+        if rows < flat_rows:
+            one = jnp.concatenate([one, jnp.zeros((flat_rows - rows, LANES), I32)], axis=0)
+        one = jnp.where(field == per_group, one + (src * rows_here << OWNER_SHIFT), one)
+        move = (base & (ROUND - 1)) * FIELDS
+        one = pltpu.roll(one, move, axis=1)
+        one = jnp.where(lane < move, pltpu.roll(one, 1, axis=0), one)
+        one = pltpu.roll(one, base // ROUND, axis=0)
+        joined = jnp.where((group >= base) & (group < base + size), one, joined)
+        base = base + size
+    low_bits = (1 << OWNER_SHIFT) - 1
+    last = group + ((pltpu.roll(joined, 1, axis=1) & low_bits) >> 1)
+    fresh = pltpu.roll(joined, 2, axis=1) & 1
+    values = jnp.where(field == per_group + 1, last, fresh)
+    values = jnp.where(field == per_group, joined >> OWNER_SHIFT, values)
+    flat_vmem[...] = jnp.where(field < per_group, joined >> LIVE_BITS, values)
+    to_smem = pltpu.make_async_copy(flat_vmem, flat, flat_sem)
+    to_smem.start()
+
+    live = jnp.where(field < per_group, joined & ((1 << LIVE_BITS) - 1), 0).astype(F32)
+    spread = iota((LANES, LANES), 0) % FIELDS == iota((LANES, LANES), 1) // page_rows
+    spread = jnp.where(spread, 1.0, 0.0).astype(BF16)
+    chosen = iota((ROUND, LANES), 1) // FIELDS == iota((ROUND, LANES), 0)
     token_row = ((iota((1, LANES), 1) % page_rows) // kv_local).astype(F32)
-    for src in range(sources):
-        live = (info_all[src] & ((1 << LIVE_BITS) - 1)).astype(F32)
-        picks = [jnp.where(chosen, live[b : b + 1], 0.0) for b in range(slot_rows)]
-        wide = nn(jnp.concatenate(picks, axis=0).astype(BF16), spread)
-        rows = slice(src * slot_rows * per_row, (src + 1) * slot_rows * per_row)
-        bias[rows, 0, :] = jnp.where(token_row < wide, 0.0, FLOOR)
+    picks = [jnp.where(chosen, live[b : b + 1], 0.0) for b in range(steps)]
+    wide = nn(jnp.concatenate(picks, axis=0).astype(BF16), spread)
+    bias[:, 0, :] = jnp.where(token_row < wide, 0.0, FLOOR)
+    to_smem.wait()
 
     q_relay()
     q_arrive()
@@ -356,14 +356,14 @@
         return by_page([jnp.broadcast_to(ref[p], (SUB, LANES)) for p in page_ids])
 
     def same_owner(it, j):
-        return jnp.full((heads, LANES), flat[it, j * FIELDS + 6], I32) > 0
+        return jnp.full((heads, LANES), flat[it, j * FIELDS + per_group + 2], I32) == 0
 
     def score_step(it, top):
         for pair in range(ROUND // 2):
             js = (2 * pair, 2 * pair + 1)
             ids = [[flat[it, j * FIELDS + i] for i in range(per_group)] for j in js]
             kk = jnp.concatenate([fetch(k_buf, one) for one in ids], axis=1)
-            qa, qb = [q_all[flat[it, j * FIELDS + 4]] for j in js]
+            qa, qb = [q_all[flat[it, j * FIELDS + per_group]] for j in js]
             lhs = jnp.concatenate(
                 [jnp.concatenate([qa, blank], axis=1), jnp.concatenate([blank, qb], axis=1)], axis=0
             )
@@ -371,7 +371,7 @@
             for x, j in enumerate(js):
                 g = it * ROUND + j
                 scale = scale_row(kse, ids[x])
-                shift = jnp.broadcast_to(bias[flat[it, j * FIELDS + 7]], (SUB, LANES))
+                shift = jnp.broadcast_to(bias[g], (SUB, LANES))
                 tiles = []
                 for t in range(heads // SUB):
                     tile = s[x * heads + t * SUB : x * heads + (t + 1) * SUB] * scale + shift
@@ -395,7 +395,7 @@
             vv = jnp.concatenate([fetch(v_buf, one) for one in ids], axis=1)
             lhs, weights = [], []
             for x, j in enumerate(js):
-                weight = jnp.exp(scores[it * ROUND + j] - peaks[flat[it, j * FIELDS + 5]])
+                weight = jnp.exp(scores[it * ROUND + j] - peaks[flat[it, j * FIELDS + per_group + 1]])
                 scale = scale_row(vse, ids[x])
                 scaled = [weight[t * SUB : (t + 1) * SUB] * scale for t in range(heads // SUB)]
                 lhs.append(jnp.concatenate(scaled, axis=0).astype(BF16))
@@ -419,11 +419,11 @@
     def first_group(dest):
         base = jnp.int32(0)
         for src in range(sources):
-            base = base + jnp.where(src < dest, table[src, last_row, rows_here], 0)
+            base = base + jnp.where(src < dest, marks[src, rows_here], 0)
         return base
 
     def local_part(dest, base, r):
-        mark = table[dest, last_row, r]
+        mark = marks[dest, r]
         last = base + (mark >> 1)
         some = (mark & 1).astype(F32)
         den = jnp.broadcast_to(jnp.sum(dens[last], axis=1, keepdims=True), (heads, LANES))
@@ -585,13 +585,13 @@
     requests = rows_here * sources
     page_rows = page_size * kv_local
     per_group = LANES // page_rows
-    group_bound = (pages + (per_group - 1) * requests) // per_group + sources
+    group_bound = (pages + (per_group - 1) * requests) // per_group
     n_groups = -(-group_bound // ROUND) * ROUND
     list_bound = (pages + (per_group - 1) * rows_here) // per_group
-    slot_rows = -(-list_bound * per_group // LANES)
-    group_rows = -(-list_bound // LANES)
-    info_rows = -(-(slot_rows + group_rows + 1) // SUB) * SUB
-    table_rows = -(-(slot_rows + 2 * group_rows + 1) // SUB) * SUB
+    list_rows = -(-list_bound // ROUND)
+    info_rows = -(-(list_rows + 1) // SUB) * SUB
+    flat_rows = -(-(n_groups // ROUND) // SUB) * SUB
+    mark_rows = -(-sources // SUB) * SUB
     chips = sources // 2
     k_rows = k_codes.reshape(pages, page_rows, dim)
     v_rows = value_quantized_codes.reshape(pages, page_rows, dim)
@@ -608,8 +608,7 @@
         page_size=page_size,
         n_groups=n_groups,
         per_group=per_group,
-        slot_rows=slot_rows,
-        group_rows=group_rows,
+        list_rows=list_rows,
     )
     vmem = pl.BlockSpec(memory_space=pltpu.VMEM)
     smem = pl.BlockSpec(memory_space=pltpu.SMEM)
@@ -629,16 +628,17 @@
         out_specs=vmem,
         scratch_shapes=[
             pltpu.VMEM(info.shape, I32),
-            pltpu.VMEM((sources, table_rows, LANES), I32),
-            pltpu.SMEM((sources, table_rows, LANES), I32),
-            pltpu.SMEM((n_groups // ROUND, LANES), I32),
+            pltpu.VMEM((mark_rows, LANES), I32),
+            pltpu.SMEM((mark_rows, LANES), I32),
+            pltpu.VMEM((flat_rows, LANES), I32),
+            pltpu.SMEM((flat_rows, LANES), I32),
             pltpu.VMEM((requests, heads, dim), BF16),
             pltpu.VMEM(k_rows.shape, BF16),
             pltpu.VMEM(v_rows.shape, BF16),
             pltpu.VMEM(out_weight.shape, BF16),
             pltpu.VMEM((pages, 1, LANES), F32),
             pltpu.VMEM((pages, 1, LANES), F32),
-            pltpu.VMEM((sources * slot_rows * (LANES // per_group), 1, LANES), F32),
+            pltpu.VMEM((n_groups, 1, LANES), F32),
             pltpu.VMEM((n_groups, heads, LANES), F32),
             pltpu.VMEM((n_groups, heads, LANES), F32),
             pltpu.VMEM((n_groups, heads, LANES), F32),
@@ -657,6 +657,7 @@
             pltpu.VMEM((nz, requests, columns // nz), BF16),
             dma,
             dma((3, 4)),
+            dma,
             dma,
             dma,
             dma((sources,)),

time: 69 us -> 53 us (0.77)
  Pallas kernels: 67.3 us -> 51.3 us
    pallas_call x1, Pallas kernels: 65 us -> 48.8 us  [on_device(): pl.pallas_call(functools.partial(kernel, cfg), out_shape=jax.ShapeDtypeSt...]
where the time goes in v3:
time: 53 us; the launch traced here: 52.8 us
  Pallas kernels  51.3 us (97%)
  local copies, waits for them, and re-layouts  1.47 us (3%)
    pallas_call x1, Pallas kernels, on_device(): pl.pallas_call(functools.partial(kernel, cfg), out_shape=jax.ShapeDtypeSt...  48.8 us
    pallas_call x1, Pallas kernels, on_device(): pl.pallas_call(functools.partial(list_kernel, cfg), out_shape=jax.ShapeDt...  2.44 us
    unnamed x1, local copies, waits for them, and re-layouts  1.47 us

profile of v3, /device:TPU:0, one launch (start us, length us, event | category | flops | bytes accessed | tf_op | source)
XLA Modules:
  0.0 52.8 jit_solution(2054557690516885726)
XLA Ops:
  0.0 2.4 %lists.1.info_ref = s32[8,24,128]{2,1,0:T(8,128)} custom-call(s32[16]{0:T(128)} %lengths_ref.1, s32[16,128]{1,0:T(8,128)} %table_ref.1), custom_call_target="tpu_custom_call" | custom-call | tf_op jit(solution)/shard_map/lists/pallas_call | solution.py:617
  2.4 48.8 %paged.1 = bf16[128,256]{1,0:T(8,128)(2,1)} custom-call(s32[8,24,128]{2,1,0:T(8,128)} %lists.1.info_ref, f32[2,1024]{1,0:T(2,128)} %bitcast.6, f32[2,1024]{1,0:T(2,128)} %bitcast.7, bf16[16,16,128]{2,1,0:T(8,128)(2,1)} %q_hbm.1, bf16[1024,32,128]{2,1,0:T(8,128)(2,1)} %bitcast.4, bf16[1024,32,128]{2,1,0:T(8,128)(2,1)} %bitcast.5, bf16[2048,1024]{1,0:T(8,128)(2,1)} %w_hbm.1), custom_call_target="tpu_custom_call" | custom-call | tf_op jit(solution)/shard_map/paged/pallas_call | solution.py:624
  51.3 1.5 %copy.10 = bf16[128,256]{1,0:T(8,128)(2,1)} copy(bf16[128,256]{1,0:T(8,128)(2,1)} %paged.1) | data formatting | bytes 131072

commit v4 on v3

--- a/solution.py
+++ b/solution.py
@@ -108,14 +108,17 @@
 
 def kernel(
     cfg,
-    info_ref,
-    kscale_ref,
-    vscale_ref,
+    info_hbm,
+    kscale_hbm,
+    vscale_hbm,
     q_hbm,
     k_hbm,
     v_hbm,
     w_hbm,
     out_ref,
+    info_ref,
+    kscale_ref,
+    vscale_ref,
     info_all,
     mark_vmem,
     marks,
@@ -144,9 +147,11 @@
     att_all,
     term_send,
     term_recv,
+    own_terms,
     q_sem,
     load_sems,
     info_sem,
+    small_sems,
     mark_sem,
     flat_sem,
     t_send,
@@ -190,10 +195,23 @@
     list_rows = cfg["list_rows"]
     flat_rows = flat_vmem.shape[0]
 
+    barrier = pltpu.get_barrier_semaphore()
+    for k in range(1, sources):
+        pl.semaphore_signal(
+            barrier, inc=1, device_id={"req": lax.rem(me + k, sources)}, device_id_type=MESH
+        )
+    for k in range(1, nz):
+        pl.semaphore_signal(barrier, inc=1, device_id={"head": lax.rem(mz + k, nz)}, device_id_type=MESH)
     q_load = pltpu.make_async_copy(q_hbm, q_all.at[pl.ds(me * rows_here, rows_here)], q_sem)
     q_load.start()
-    info_load = pltpu.make_async_copy(info_ref.at[me], info_all.at[me], info_sem)
+    info_load = pltpu.make_async_copy(info_hbm.at[me], info_all.at[me], info_sem)
     info_load.start()
+    smalls = []
+    pairs = ((info_hbm, info_ref), (kscale_hbm, kscale_ref), (vscale_hbm, vscale_ref))
+    for n, (src, dst) in enumerate(pairs):
+        cp = pltpu.make_async_copy(src, dst, small_sems.at[n])
+        cp.start()
+        smalls.append(cp)
     loads = []
     parts = load_sems.shape[1]
     for which, (src, dst) in enumerate(((k_hbm, k_buf), (v_hbm, v_buf), (w_hbm, w_buf))):
@@ -205,13 +223,6 @@
             loads.append(cp)
     k_loads, v_loads, w_loads = loads[:parts], loads[parts : 2 * parts], loads[2 * parts :]
 
-    barrier = pltpu.get_barrier_semaphore()
-    for k in range(1, sources):
-        pl.semaphore_signal(
-            barrier, inc=1, device_id={"req": lax.rem(me + k, sources)}, device_id_type=MESH
-        )
-    for k in range(1, nz):
-        pl.semaphore_signal(barrier, inc=1, device_id={"head": lax.rem(mz + k, nz)}, device_id_type=MESH)
     pl.semaphore_wait(barrier, sources + nz - 2)
 
     def info_copy(peer, owner):
@@ -246,16 +257,16 @@
                 direct(other_chip(k) * 2 + core, me).start()
             direct(partner, me).start()
 
-        def relay():
-            for k in far:
-                owner = other_chip(k) * 2 + core
-                direct(owner, owner).wait_recv()
-                onward(owner).start()
-
-        def arrive():
-            direct(partner, partner).wait_recv()
-            for k in far:
-                owner = other_chip(k) * 2 + 1 - core
+        def pass_on(k):
+            owner = other_chip(k) * 2 + core
+            direct(owner, owner).wait_recv()
+            onward(owner).start()
+
+        def take(k):
+            owner = other_chip(k) * 2 + 1 - core
+            if k == 0:
+                direct(partner, partner).wait_recv()
+            else:
                 onward(owner).wait_recv()
 
         def finish():
@@ -265,16 +276,19 @@
                 direct(owner, me).wait_send()
                 onward(owner).wait_send()
 
-        return begin, relay, arrive, finish
-
-    q_begin, q_relay, q_arrive, q_finish = gather(
+        return begin, pass_on, take, finish
+
+    q_begin, q_pass_on, q_take, q_finish = gather(
         lambda owner: q_all.at[pl.ds(owner * rows_here, rows_here)], q_send, q_recv, q_pass
     )
+    smalls[0].wait()
     for k in range(sources - 1, 0, -1):
         info_copy(lax.rem(me + k, sources), me).start()
     q_load.wait()
     q_begin()
 
+    for cp in smalls[1:]:
+        cp.wait()
     lane_sub = iota((LANES, LANES), 0)
     for src, dst, factor in ((kscale_ref, kse, 1.0 / math.sqrt(dim)), (vscale_ref, vse, 1.0)):
         for b in range(pages // LANES):
@@ -332,8 +346,10 @@
     bias[:, 0, :] = jnp.where(token_row < wide, 0.0, FLOOR)
     to_smem.wait()
 
-    q_relay()
-    q_arrive()
+    for k in far:
+        q_pass_on(k)
+    for k in range(chips):
+        q_take(k)
     for cp in k_loads:
         cp.wait()
 
@@ -511,47 +527,53 @@
         rows = mixed[pl.ds(h, rows_here, stride=heads), :]
         att_all[me, :, h * dim : (h + 1) * dim] = rows.astype(BF16)
 
-    a_begin, a_relay, a_arrive, a_finish = gather(lambda owner: att_all.at[owner], a_send, a_recv, a_pass)
+    a_begin, a_pass_on, a_take, a_finish = gather(lambda owner: att_all.at[owner], a_send, a_recv, a_pass)
     a_begin()
     for cp in w_loads:
         cp.wait()
-    a_relay()
-    a_arrive()
-
-    att = att_all[...].reshape(requests, width)
+
     cols = w_buf.shape[1] // nz
-
-    def term_copy(peer, owner):
-        return pltpu.make_async_remote_copy(
-            src_ref=term_send.at[peer],
-            dst_ref=term_recv.at[owner],
-            send_sem=z_send.at[peer],
-            recv_sem=z_recv.at[owner],
-            device_id={"head": peer},
-            device_id_type=MESH,
+    block_rows = 2 * rows_here
+
+    def term_copy(to, owner, c):
+        return remote(
+            term_send.at[to, c], term_recv.at[owner, c], z_send.at[to, c], z_recv.at[owner, c], head=to
         )
 
-    def project(z):
-        return nn(att, w_buf[:, pl.ds(pl.multiple_of(z * cols, cols), cols)])
-
-    if cols % LANES == 0:
-        for k in range(1, nz):
-            peer = lax.rem(mz + k, nz)
-            term_send[peer] = project(peer).astype(BF16)
-            term_copy(peer, mz).start()
-        result = project(mz)
-    else:
-        every = nn(att, w_buf[...])
-        for z in range(nz):
-            term_send[z] = every[:, z * cols : (z + 1) * cols].astype(BF16)
-        for k in range(1, nz):
-            term_copy(lax.rem(mz + k, nz), mz).start()
-        result = term_send[mz].astype(F32)
-    for k in range(1, nz):
-        peer = lax.rem(mz + k, nz)
-        term_copy(peer, peer).wait_recv()
-        result = result + term_recv[peer].astype(F32)
-    out_ref[...] = result.astype(BF16)
+    def project(c):
+        att = att_all[pl.ds(2 * c, 2)].reshape(block_rows, width)
+        if cols % LANES == 0:
+            for k in range(1, nz):
+                peer = lax.rem(mz + k, nz)
+                columns = pl.ds(pl.multiple_of(peer * cols, cols), cols)
+                term_send[peer, c] = nn(att, w_buf[:, columns]).astype(BF16)
+                term_copy(peer, mz, c).start()
+            own_terms[c] = nn(att, w_buf[:, pl.ds(pl.multiple_of(mz * cols, cols), cols)])
+        else:
+            every = nn(att, w_buf[...])
+            for z in range(nz):
+                term_send[z, c] = every[:, z * cols : (z + 1) * cols].astype(BF16)
+            for k in range(1, nz):
+                term_copy(lax.rem(mz + k, nz), mz, c).start()
+            own_terms[c] = term_send[mz, c].astype(F32)
+
+    order = sorted(range(1, chips), key=lambda k: (k % 2, k))
+    a_take(0)
+    ready = 0
+    for k in order:
+        a_pass_on(k)
+        project(other_chip(ready))
+        a_take(k)
+        ready = k
+    project(other_chip(ready))
+    for k in [0] + order:
+        c = other_chip(k)
+        got = own_terms[c]
+        for z in range(1, nz):
+            peer = lax.rem(mz + z, nz)
+            term_copy(peer, peer, c).wait_recv()
+            got = got + term_recv[peer, c].astype(F32)
+        out_ref[pl.ds(pl.multiple_of(c * block_rows, block_rows), block_rows), :] = got.astype(BF16)
 
     for k in range(1, sources):
         peer = lax.rem(me + k, sources)
@@ -566,7 +588,8 @@
         num_copy(c, chip).wait_send()
         lse_copy(c, chip).wait_send()
     for k in range(1, nz):
-        term_copy(lax.rem(mz + k, nz), mz).wait_send()
+        for c in range(chips):
+            term_copy(lax.rem(mz + k, nz), mz, c).wait_send()
 
 
 def on_device(
@@ -624,9 +647,12 @@
     return pl.pallas_call(
         functools.partial(kernel, cfg),
         out_shape=jax.ShapeDtypeStruct((requests, columns // nz), BF16),
-        in_specs=[vmem, vmem, vmem, hbm, hbm, hbm, hbm],
+        in_specs=[hbm] * 7,
         out_specs=vmem,
         scratch_shapes=[
+            pltpu.VMEM(info.shape, I32),
+            pltpu.VMEM((kv_local, pages), F32),
+            pltpu.VMEM((kv_local, pages), F32),
             pltpu.VMEM(info.shape, I32),
             pltpu.VMEM((mark_rows, LANES), I32),
             pltpu.SMEM((mark_rows, LANES), I32),
@@ -653,11 +679,13 @@
             pltpu.VMEM((chips, heads, LANES), F32),
             pltpu.VMEM((rows_here * heads, dim), F32),
             pltpu.VMEM((sources, rows_here, width), BF16),
-            pltpu.VMEM((nz, requests, columns // nz), BF16),
-            pltpu.VMEM((nz, requests, columns // nz), BF16),
+            pltpu.VMEM((nz, chips, 2 * rows_here, columns // nz), BF16),
+            pltpu.VMEM((nz, chips, 2 * rows_here, columns // nz), BF16),
+            pltpu.VMEM((chips, 2 * rows_here, columns // nz), F32),
             dma,
             dma((3, 4)),
             dma,
+            dma((3,)),
             dma,
             dma,
             dma((sources,)),
@@ -676,8 +704,8 @@
             dma((sources,)),
             dma((sources,)),
             dma((sources,)),
-            dma((nz,)),
-            dma((nz,)),
+            dma((nz, chips)),
+            dma((nz, chips)),
         ],
         compiler_params=pltpu.CompilerParams(
             vmem_limit_bytes=62 * 1024 * 1024, collective_id=0, has_side_effects=True

time: 53 us -> 57.6 us (1.087)
  Pallas kernels: 51.3 us -> 55.9 us
    pallas_call x1, Pallas kernels: 48.8 us -> 53.5 us  [on_device(): pl.pallas_call(functools.partial(kernel, cfg), out_shape=jax.ShapeDtypeSt...]
where the time goes in v4:
time: 57.6 us; the launch traced here: 57.4 us
  Pallas kernels  55.9 us (97%)
  local copies, waits for them, and re-layouts  1.47 us (3%)
    pallas_call x1, Pallas kernels, on_device(): pl.pallas_call(functools.partial(kernel, cfg), out_shape=jax.ShapeDtypeSt...  53.5 us
    pallas_call x1, Pallas kernels, on_device(): pl.pallas_call(functools.partial(list_kernel, cfg), out_shape=jax.ShapeDt...  2.44 us
    unnamed x1, local copies, waits for them, and re-layouts  1.47 us

profile of v4, /device:TPU:0, one launch (start us, length us, event | category | flops | bytes accessed | tf_op | source)
XLA Modules:
  0.0 57.4 jit_solution(6078852400514539826)
XLA Ops:
  0.0 2.4 %lists.1.info_hbm = s32[8,24,128]{2,1,0:T(8,128)} custom-call(s32[16]{0:T(128)} %lengths_ref.1, s32[16,128]{1,0:T(8,128)} %table_ref.1), custom_call_target="tpu_custom_call" | custom-call | tf_op jit(solution)/shard_map/lists/pallas_call | solution.py:640
  2.4 53.5 %paged.1 = bf16[128,256]{1,0:T(8,128)(2,1)} custom-call(s32[8,24,128]{2,1,0:T(8,128)} %lists.1.info_hbm, f32[2,1024]{1,0:T(2,128)} %bitcast.6, f32[2,1024]{1,0:T(2,128)} %bitcast.7, bf16[16,16,128]{2,1,0:T(8,128)(2,1)} %q_hbm.1, bf16[1024,32,128]{2,1,0:T(8,128)(2,1)} %bitcast.4, bf16[1024,32,128]{2,1,0:T(8,128)(2,1)} %bitcast.5, bf16[2048,1024]{1,0:T(8,128)(2,1)} %w_hbm.1), custom_call_target="tpu_custom_call" | custom-call | tf_op jit(solution)/shard_map/paged/pallas_call | solution.py:647
  55.9 1.5 %copy.10 = bf16[128,256]{1,0:T(8,128)(2,1)} copy(bf16[128,256]{1,0:T(8,128)(2,1)} %paged.1) | data formatting | bytes 131072

commit v5 on v4

--- a/solution.py
+++ b/solution.py
@@ -212,6 +212,72 @@
         cp = pltpu.make_async_copy(src, dst, small_sems.at[n])
         cp.start()
         smalls.append(cp)
+
+    pl.semaphore_wait(barrier, sources + nz - 2)
+
+    def info_copy(peer, owner):
+        return pltpu.make_async_remote_copy(
+            src_ref=info_ref.at[peer],
+            dst_ref=info_all.at[owner],
+            send_sem=t_send.at[peer],
+            recv_sem=t_recv.at[owner],
+            device_id={"req": peer},
+            device_id_type=MESH,
+        )
+
+    def remote(src, dst, send, recv, **where):
+        return pltpu.make_async_remote_copy(
+            src_ref=src,
+            dst_ref=dst,
+            send_sem=send,
+            recv_sem=recv,
+            device_id=where,
+            device_id_type=MESH,
+        )
+
+    def gather(rows_of, send, recv, passing):
+        def direct(peer, owner):
+            return remote(rows_of(owner), rows_of(owner), send.at[peer], recv.at[owner], req=peer)
+
+        def onward(owner):
+            return remote(rows_of(owner), rows_of(owner), passing.at[owner], recv.at[owner], req=partner)
+
+        def begin():
+            for k in far:
+                direct(other_chip(k) * 2 + core, me).start()
+            direct(partner, me).start()
+
+        def pass_on(k):
+            owner = other_chip(k) * 2 + core
+            direct(owner, owner).wait_recv()
+            onward(owner).start()
+
+        def take(k):
+            owner = other_chip(k) * 2 + 1 - core
+            if k == 0:
+                direct(partner, partner).wait_recv()
+            else:
+                onward(owner).wait_recv()
+
+        def finish():
+            direct(partner, me).wait_send()
+            for k in far:
+                owner = other_chip(k) * 2 + core
+                direct(owner, me).wait_send()
+                onward(owner).wait_send()
+
+        return begin, pass_on, take, finish
+
+    q_begin, q_pass_on, q_take, q_finish = gather(
+        lambda owner: q_all.at[pl.ds(owner * rows_here, rows_here)], q_send, q_recv, q_pass
+    )
+    smalls[0].wait()
+    for k in range(sources - 1, 0, -1):
+        info_copy(lax.rem(me + k, sources), me).start()
+    q_load.wait()
+    for cp in smalls[1:]:
+        cp.wait()
+    q_begin()
     loads = []
     parts = load_sems.shape[1]
     for which, (src, dst) in enumerate(((k_hbm, k_buf), (v_hbm, v_buf), (w_hbm, w_buf))):
@@ -223,72 +289,6 @@
             loads.append(cp)
     k_loads, v_loads, w_loads = loads[:parts], loads[parts : 2 * parts], loads[2 * parts :]
 
-    pl.semaphore_wait(barrier, sources + nz - 2)
-
-    def info_copy(peer, owner):
-        return pltpu.make_async_remote_copy(
-            src_ref=info_ref.at[peer],
-            dst_ref=info_all.at[owner],
-            send_sem=t_send.at[peer],
-            recv_sem=t_recv.at[owner],
-            device_id={"req": peer},
-            device_id_type=MESH,
-        )
-
-    def remote(src, dst, send, recv, **where):
-        return pltpu.make_async_remote_copy(
-            src_ref=src,
-            dst_ref=dst,
-            send_sem=send,
-            recv_sem=recv,
-            device_id=where,
-            device_id_type=MESH,
-        )
-
-    def gather(rows_of, send, recv, passing):
-        def direct(peer, owner):
-            return remote(rows_of(owner), rows_of(owner), send.at[peer], recv.at[owner], req=peer)
-
-        def onward(owner):
-            return remote(rows_of(owner), rows_of(owner), passing.at[owner], recv.at[owner], req=partner)
-
-        def begin():
-            for k in far:
-                direct(other_chip(k) * 2 + core, me).start()
-            direct(partner, me).start()
-
-        def pass_on(k):
-            owner = other_chip(k) * 2 + core
-            direct(owner, owner).wait_recv()
-            onward(owner).start()
-
-        def take(k):
-            owner = other_chip(k) * 2 + 1 - core
-            if k == 0:
-                direct(partner, partner).wait_recv()
-            else:
-                onward(owner).wait_recv()
-
-        def finish():
-            direct(partner, me).wait_send()
-            for k in far:
-                owner = other_chip(k) * 2 + core
-                direct(owner, me).wait_send()
-                onward(owner).wait_send()
-
-        return begin, pass_on, take, finish
-
-    q_begin, q_pass_on, q_take, q_finish = gather(
-        lambda owner: q_all.at[pl.ds(owner * rows_here, rows_here)], q_send, q_recv, q_pass
-    )
-    smalls[0].wait()
-    for k in range(sources - 1, 0, -1):
-        info_copy(lax.rem(me + k, sources), me).start()
-    q_load.wait()
-    q_begin()
-
-    for cp in smalls[1:]:
-        cp.wait()
     lane_sub = iota((LANES, LANES), 0)
     for src, dst, factor in ((kscale_ref, kse, 1.0 / math.sqrt(dim)), (vscale_ref, vse, 1.0)):
         for b in range(pages // LANES):
@@ -540,32 +540,38 @@
             term_send.at[to, c], term_recv.at[owner, c], z_send.at[to, c], z_recv.at[owner, c], head=to
         )
 
-    def project(c):
-        att = att_all[pl.ds(2 * c, 2)].reshape(block_rows, width)
+    def project(picked):
+        att = [att_all[pl.ds(2 * c, 2)].reshape(block_rows, width) for c in picked]
+        att = jnp.concatenate(att, axis=0)
+        spans = [slice(i * block_rows, (i + 1) * block_rows) for i in range(len(picked))]
         if cols % LANES == 0:
             for k in range(1, nz):
                 peer = lax.rem(mz + k, nz)
                 columns = pl.ds(pl.multiple_of(peer * cols, cols), cols)
-                term_send[peer, c] = nn(att, w_buf[:, columns]).astype(BF16)
-                term_copy(peer, mz, c).start()
-            own_terms[c] = nn(att, w_buf[:, pl.ds(pl.multiple_of(mz * cols, cols), cols)])
+                term = nn(att, w_buf[:, columns]).astype(BF16)
+                for c, span in zip(picked, spans):
+                    term_send[peer, c] = term[span]
+                    term_copy(peer, mz, c).start()
+            term = nn(att, w_buf[:, pl.ds(pl.multiple_of(mz * cols, cols), cols)])
+            for c, span in zip(picked, spans):
+                own_terms[c] = term[span]
         else:
             every = nn(att, w_buf[...])
-            for z in range(nz):
-                term_send[z, c] = every[:, z * cols : (z + 1) * cols].astype(BF16)
-            for k in range(1, nz):
-                term_copy(lax.rem(mz + k, nz), mz, c).start()
-            own_terms[c] = term_send[mz, c].astype(F32)
-
-    order = sorted(range(1, chips), key=lambda k: (k % 2, k))
+            for c, span in zip(picked, spans):
+                for z in range(nz):
+                    term_send[z, c] = every[span, z * cols : (z + 1) * cols].astype(BF16)
+                for k in range(1, nz):
+                    term_copy(lax.rem(mz + k, nz), mz, c).start()
+                own_terms[c] = term_send[mz, c].astype(F32)
+
+    order = list(range(1, chips))
     a_take(0)
-    ready = 0
+    project([other_chip(0)])
     for k in order:
         a_pass_on(k)
-        project(other_chip(ready))
+    for k in order:
         a_take(k)
-        ready = k
-    project(other_chip(ready))
+    project([other_chip(k) for k in order])
     for k in [0] + order:
         c = other_chip(k)
         got = own_terms[c]

time: 57.6 us -> 51.2 us (0.89)
  Pallas kernels: 55.9 us -> 49.5 us
    pallas_call x1, Pallas kernels: 53.5 us -> 47 us  [on_device(): pl.pallas_call(functools.partial(kernel, cfg), out_shape=jax.ShapeDtypeSt...]
where the time goes in v5:
time: 51.2 us; the launch traced here: 51 us
  Pallas kernels  49.5 us (97%)
  local copies, waits for them, and re-layouts  1.47 us (3%)
    pallas_call x1, Pallas kernels, on_device(): pl.pallas_call(functools.partial(kernel, cfg), out_shape=jax.ShapeDtypeSt...  47 us
    pallas_call x1, Pallas kernels, on_device(): pl.pallas_call(functools.partial(list_kernel, cfg), out_shape=jax.ShapeDt...  2.44 us
    unnamed x1, local copies, waits for them, and re-layouts  1.47 us

profile of v5, /device:TPU:0, one launch (start us, length us, event | category | flops | bytes accessed | tf_op | source)
XLA Modules:
  0.0 51.0 jit_solution(13288671163518315462)
XLA Ops:
  0.0 2.4 %lists.1.info_hbm = s32[8,24,128]{2,1,0:T(8,128)} custom-call(s32[16]{0:T(128)} %lengths_ref.1, s32[16,128]{1,0:T(8,128)} %table_ref.1), custom_call_target="tpu_custom_call" | custom-call | tf_op jit(solution)/shard_map/lists/pallas_call | solution.py:646
  2.4 47.0 %paged.1 = bf16[128,256]{1,0:T(8,128)(2,1)} custom-call(s32[8,24,128]{2,1,0:T(8,128)} %lists.1.info_hbm, f32[2,1024]{1,0:T(2,128)} %bitcast.6, f32[2,1024]{1,0:T(2,128)} %bitcast.7, bf16[16,16,128]{2,1,0:T(8,128)(2,1)} %q_hbm.1, bf16[1024,32,128]{2,1,0:T(8,128)(2,1)} %bitcast.4, bf16[1024,32,128]{2,1,0:T(8,128)(2,1)} %bitcast.5, bf16[2048,1024]{1,0:T(8,128)(2,1)} %w_hbm.1), custom_call_target="tpu_custom_call" | custom-call | tf_op jit(solution)/shard_map/paged/pallas_call | solution.py:653
  49.5 1.5 %copy.10 = bf16[128,256]{1,0:T(8,128)(2,1)} copy(bf16[128,256]{1,0:T(8,128)(2,1)} %paged.1) | data formatting | bytes 131072

commit v6 on v5

--- a/solution.py
+++ b/solution.py
@@ -305,9 +305,9 @@
         info_copy(peer, peer).wait_recv()
     for src in range(sources):
         mark_vmem[src : src + 1, :] = info_all[src, list_rows : list_rows + 1, :]
-    to_smem = pltpu.make_async_copy(mark_vmem, marks, mark_sem)
-    to_smem.start()
-    to_smem.wait()
+    to_marks = pltpu.make_async_copy(mark_vmem, marks, mark_sem)
+    to_marks.start()
+    size_lane = iota((1, LANES), 1) == rows_here
 
     shape = (flat_rows, LANES)
     lane, field = iota(shape, 1), iota(shape, 1) % FIELDS
@@ -315,7 +315,7 @@
     joined = jnp.zeros(shape, I32)
     base = jnp.int32(0)
     for src in range(sources):
-        size = marks[src, rows_here]
+        size = jnp.sum(jnp.where(size_lane, info_all[src, list_rows : list_rows + 1, :], 0))
         rows = min(flat_rows, info_all.shape[1])
         one = info_all[src, :rows, :]
         if rows < flat_rows:
@@ -345,6 +345,7 @@
     wide = nn(jnp.concatenate(picks, axis=0).astype(BF16), spread)
     bias[:, 0, :] = jnp.where(token_row < wide, 0.0, FLOOR)
     to_smem.wait()
+    to_marks.wait()
 
     for k in far:
         q_pass_on(k)
@@ -373,6 +374,9 @@
 
     def same_owner(it, j):
         return jnp.full((heads, LANES), flat[it, j * FIELDS + per_group + 2], I32) == 0
+
+    def peak_of(g):
+        return jnp.broadcast_to(jnp.max(peaks[g], axis=1, keepdims=True), (heads, LANES))
 
     def score_step(it, top):
         for pair in range(ROUND // 2):
@@ -394,8 +398,7 @@
                     tiles.append(jnp.where(kv_masks[t], tile, FLOOR))
                 tile = jnp.concatenate(tiles, axis=0)
                 scores[g] = tile
-                mine = jnp.broadcast_to(jnp.max(tile, axis=1, keepdims=True), (heads, LANES))
-                top = jnp.where(same_owner(it, j), jnp.maximum(top, mine), mine)
+                top = jnp.where(same_owner(it, j), jnp.maximum(top, tile), tile)
                 peaks[g] = top
         return top
 
@@ -411,7 +414,7 @@
             vv = jnp.concatenate([fetch(v_buf, one) for one in ids], axis=1)
             lhs, weights = [], []
             for x, j in enumerate(js):
-                weight = jnp.exp(scores[it * ROUND + j] - peaks[flat[it, j * FIELDS + per_group + 1]])
+                weight = jnp.exp(scores[it * ROUND + j] - peak_of(flat[it, j * FIELDS + per_group + 1]))
                 scale = scale_row(vse, ids[x])
                 scaled = [weight[t * SUB : (t + 1) * SUB] * scale for t in range(heads // SUB)]
                 lhs.append(jnp.concatenate(scaled, axis=0).astype(BF16))
@@ -445,7 +448,7 @@
         den = jnp.broadcast_to(jnp.sum(dens[last], axis=1, keepdims=True), (heads, LANES))
         den = jnp.maximum(den, 0.5)
         num = accs[last] * (some / den)
-        return num, (peaks[last] + jnp.log(den)) * some + (some - 1.0) * (-FLOOR)
+        return num, (peak_of(last) + jnp.log(den)) * some + (some - 1.0) * (-FLOOR)
 
     def pair_copy(c):
         return remote(pair_send.at[c], pair_recv.at[c], p_send.at[c], p_recv.at[c], req=partner)

time: 51.2 us -> 49.7 us (0.971)
  Pallas kernels: 49.5 us -> 47.8 us
    pallas_call x1, Pallas kernels: 47 us -> 45.4 us  [on_device(): pl.pallas_call(functools.partial(kernel, cfg), out_shape=jax.ShapeDtypeSt...]
where the time goes in v6:
time: 49.7 us; the launch traced here: 49.3 us
  Pallas kernels  47.8 us (96%)
  local copies, waits for them, and re-layouts  1.47 us (3%)
    pallas_call x1, Pallas kernels, on_device(): pl.pallas_call(functools.partial(kernel, cfg), out_shape=jax.ShapeDtypeSt...  45.4 us
    pallas_call x1, Pallas kernels, on_device(): pl.pallas_call(functools.partial(list_kernel, cfg), out_shape=jax.ShapeDt...  2.44 us
    unnamed x1, local copies, waits for them, and re-layouts  1.47 us

profile of v6, /device:TPU:0, one launch (start us, length us, event | category | flops | bytes accessed | tf_op | source)
XLA Modules:
  0.0 49.3 jit_solution(13716224040045819023)
XLA Ops:
  0.0 2.4 %lists.1.info_hbm = s32[8,24,128]{2,1,0:T(8,128)} custom-call(s32[16]{0:T(128)} %lengths_ref.1, s32[16,128]{1,0:T(8,128)} %table_ref.1), custom_call_target="tpu_custom_call" | custom-call | tf_op jit(solution)/shard_map/lists/pallas_call | solution.py:649
  2.4 45.4 %paged.1 = bf16[128,256]{1,0:T(8,128)(2,1)} custom-call(s32[8,24,128]{2,1,0:T(8,128)} %lists.1.info_hbm, f32[2,1024]{1,0:T(2,128)} %bitcast.6, f32[2,1024]{1,0:T(2,128)} %bitcast.7, bf16[16,16,128]{2,1,0:T(8,128)(2,1)} %q_hbm.1, bf16[1024,32,128]{2,1,0:T(8,128)(2,1)} %bitcast.4, bf16[1024,32,128]{2,1,0:T(8,128)(2,1)} %bitcast.5, bf16[2048,1024]{1,0:T(8,128)(2,1)} %w_hbm.1), custom_call_target="tpu_custom_call" | custom-call | tf_op jit(solution)/shard_map/paged/pallas_call | solution.py:656
  47.8 1.5 %copy.10 = bf16[128,256]{1,0:T(8,128)(2,1)} copy(bf16[128,256]{1,0:T(8,128)(2,1)} %paged.1) | data formatting | bytes 131072
